TPU v7x, 128 devices: a whole 4x4x4 slice. The times are simulated.
128 devices in a mesh: stream: 4 (over x), tm: 32 (over z, y, core).
Axes of the slice: x: 4, y: 4, z: 4, core: 2. Of those that a mesh axis runs over, the one named last changes fastest.
Arguments:
- voltages: float32 [2, 16384, 4096], P(None, ('stream', 'tm')), parts along dimension 1, may hold values from -100 to 100
- taps: float32 [16, 4096], replicated, may hold values from -1.5 to 1.5
- flags: int32 [128], P('stream'), parts along dimension 0, may hold values from 0 to 1, as said below
Outputs:
- dynamic: float32 [4096, 4096], P('stream', 'tm'), parts along dimension 0
- kurtosis: float32 [16384], P(('stream', 'tm')), parts along dimension 0
- spectrum: float32 [16384], P(('stream', 'tm')), parts along dimension 0
There are 4 independent parts, one for each index of `stream`. A program takes and returns all parts, laid end to end along the dimension named above; an argument that names none is the same for every part. Nothing has to cross between parts.
Inputs may be any that keep to these rules, and one draw needn't show every extreme that they name: `flags`: at least one and at most 16 blocks of a stream are flagged.
All inputs are finite; a program needn't handle non-finite values.
Results may differ from a plain program's by a relative error of at most 0.00016.
Values sent between devices are 32-bit elements; how exact they have to be, the bound alone decides.
A program may use at most 64 MiB of HBM per device.

v0:
```python
import math

import jax
import jax.numpy as jnp
from jax import lax
from jax.sharding import PartitionSpec as P

SUMMED = 4


def from_behind(value, axis, by):
    count = lax.axis_size(axis)
    pairs = [(i, i + by) for i in range(count) if 0 <= i + by < count]
    return lax.ppermute(value, axis, pairs)


def from_everyone(value, axis):
    count = lax.axis_size(axis)
    return lax.all_to_all(
        jnp.broadcast_to(value[None], (count, *value.shape)), axis, 0, 0, tiled=True
    )


def over_copies(value, axis):
    everything = from_everyone(value, axis)
    return jnp.sum(everything, axis=0)


def in_one(arrays, axis):
    ends = [0]
    for a in arrays:
        ends.append(ends[-1] + a.size)
    so_far = over_copies(jnp.concatenate([a.ravel() for a in arrays]), axis)
    return tuple((so_far[b:e].reshape(a.shape) for a, b, e in zip(arrays, ends, ends[1:])))


def rotation(angles):
    cosine = jnp.cos(angles)
    sine = jnp.sin(angles)
    return jnp.stack([jnp.stack([cosine, -sine], 1), jnp.stack([sine, cosine], 1)], 0)


def transform(filtered):
    frames = filtered.shape[1]
    channel_list = filtered.shape[2]
    outer_len = 1
    while 4 * outer_len * outer_len <= channel_list and outer_len < 32:
        outer_len = 2 * outer_len
    inner_len = channel_list // outer_len
    low_index = jnp.arange(outer_len, dtype=jnp.int32)
    high_index = jnp.arange(inner_len, dtype=jnp.int32)
    outer_table = rotation(
        (low_index[:, None] * high_index[None, :] % outer_len).astype(jnp.float32)
        * (2.0 * math.pi / outer_len)
    )
    twist_turn = (high_index[:, None] * high_index[None, :] % channel_list).astype(jnp.float32) * (
        2.0 * math.pi / channel_list
    )
    twist_cos = jnp.cos(twist_turn)
    twist_sin = jnp.sin(twist_turn)
    inner_table = rotation(
        (high_index[:, None] * low_index[None, :] % outer_len).astype(jnp.float32)
        * (2.0 * math.pi / outer_len)
    )
    shaped = filtered.reshape(2, frames, outer_len, inner_len)
    sectioned = jnp.einsum("sfab,satd->tfdb", shaped, outer_table, precision=lax.Precision.HIGHEST)
    twisted_real = sectioned[0] * twist_cos + sectioned[1] * twist_sin
    twisted_imag = sectioned[1] * twist_cos - sectioned[0] * twist_sin
    twisted = jnp.stack([twisted_real, twisted_imag], 0)
    result = jnp.einsum("tfdb,tbuc->ufcd", twisted, inner_table, precision=lax.Precision.HIGHEST)
    return result.reshape(2, frames, channel_list)


def body(voltages, taps, flags):
    frames = voltages.shape[1]
    channel_list = voltages.shape[2]
    tap_count = taps.shape[0]
    groups = lax.axis_size("tm")
    tail_rows = voltages[:, frames - (tap_count - 1) :, :]
    before = from_behind(tail_rows, "tm", 1)
    padded = jnp.concatenate([before, voltages], axis=1)
    filtered = jnp.zeros(voltages.shape, jnp.float32)
    for offset in range(tap_count):
        begin = tap_count - 1 - offset
        filtered = filtered + taps[offset][None, None, :] * padded[:, begin : begin + frames, :]
    spectra = transform(filtered)
    channel_powers = spectra[0] * spectra[0] + spectra[1] * spectra[1]
    block_count = flags.shape[0]
    block_width = channel_list // block_count
    clean_count = jnp.broadcast_to(
        (1 - flags).astype(jnp.float32)[:, None], (block_count, block_width)
    ).reshape(channel_list)
    frame_total = frames * groups
    local_block_width = channel_list // groups
    local_mean_power = lax.axis_index("tm") * local_block_width
    local_clean_count = lax.dynamic_slice_in_dim(clean_count, local_mean_power, local_block_width)
    local_first = jnp.sum(channel_powers, axis=0)
    local_second = jnp.sum(channel_powers * channel_powers, axis=0)
    local_rows = jnp.sum(channel_powers.reshape(frames // SUMMED, SUMMED, channel_list), axis=1)
    local_total = jnp.dot(local_rows, clean_count, precision=lax.Precision.HIGHEST)
    local_dynamic = channel_list * clean_count[None, :] * local_rows / local_total[:, None]
    dynamic = lax.all_to_all(local_dynamic, "tm", split_axis=1, concat_axis=0, tiled=True)
    all_first, all_second = in_one((local_first, local_second), "tm")
    group_sum = jnp.dot(all_first, clean_count, precision=lax.Precision.HIGHEST)
    mean_power = lax.dynamic_slice_in_dim(all_first, local_mean_power, local_block_width)
    second_moment = lax.dynamic_slice_in_dim(all_second, local_mean_power, local_block_width)
    kurtosis = (
        (frame_total + 1.0)
        / (frame_total - 1.0)
        * (frame_total * second_moment / (mean_power * mean_power) - 1.0)
    )
    spectrum = channel_list * local_clean_count * mean_power / group_sum
    return (dynamic, kurtosis, spectrum)


def solution(mesh):
    placed = (P(None, ("stream", "tm"), None), P(), P("stream"))
    return jax.shard_map(
        body,
        mesh=mesh,
        in_specs=placed,
        out_specs=(P("stream", "tm"), P(("stream", "tm")), P(("stream", "tm"))),
        check_vma=False,
    )
```

profile of v0, /device:TPU:1, one launch (start us, length us, event | category | flops | bytes accessed | tf_op | source)
XLA Modules:
  0.0 136.2 jit_solution(14175163674327846353)
XLA Ops:
  0.6 1.1 slice.122
  1.7 4.6 %collective-permute-start = (f32[2,15,4096]{2,1,0:T(8,128)S(1)}, f32[2,15,4096]{2,1,0:T(8,128)S(1)}, u32[]{:S(2)}, u32[]{:S(2)}) collective-permute-start(f32[2,15,4096]{2,1,0:T(8,128)S(1)} %slice.122), channel_id=1, source_target_pairs={{0,1},{1,2},{2,3},{3,4},{4,5},{5,6},{6,7},{7,8},{8,9},{9,10},{10,1... | collective-permute-start | bytes 1474568 | tf_op jit(solution)/shard_map/ppermute | solution.py:14
  6.3 0.1 fusion.78
  6.4 0.1 fusion.83
  6.5 0.3 fusion.64
  6.8 0.1 fusion.80
  6.9 0.1 fusion.82
  6.9 2.6 %fusion.88 = (f32[1,4096]{1,0:T(1,128)S(1)}, f32[1,4096]{1,0:T(1,128)S(1)}, f32[1,4096]{1,0:T(1,128)S(1)}, f32[1,4096]{1,0:T(1,128)S(1)}, f32[1,4096]{1,0:T(1,12...) fusion(f32[16,4096]{1,0:T(8,128)} %param.4), kind=kLoop, calls=%fused_computation.146 | loop fusion | bytes 524288 | tf_op jit(solution)/shard_map/slice | solution.py:85
  9.6 0.7 subtract_convert_fusion
  10.3 0.7 broadcast_multiply_fusion
  11.0 1.5 %collective-permute-done = f32[2,15,4096]{2,1,0:T(8,128)S(1)} collective-permute-done((f32[2,15,4096]{2,1,0:T(8,128)S(1)}, f32[2,15,4096]{2,1,0:T(8,128)S(1)}, u32[]{:S(2)}, u32[]{:S(2)}) %collective-permute-start) | collective-permute-done | bytes 491552 | tf_op jit(solution)/shard_map/ppermute | solution.py:14
  12.4 29.5 %fusion.6 = f32[2,128,4096]{2,1,0:T(8,128)S(1)} fusion(f32[2,128,4096]{2,1,0:T(8,128)} %param.3, f32[2,15,4096]{2,1,0:T(8,128)S(1)} %collective-permute-done, f32[4096]{0:T(1024)S(1)} %bitcast.105, f32[4096]{0:T(1024)S(1)} %bitcast.106, f32[4096]{0:T(1024)S(1)} %bitcast.92, f32[4096]{0:T(1024)S(1)} %bitcast.93, f32[4096]{0:T(1024)S(1)} %bitcast.94, ...), kind=kLoop, calls=%fused_computation.38 | loop fusion | flops 48234496 | bytes 9142272 | tf_op jit(solution)/shard_map/add | solution.py:85
  41.9 0.8 copy.45
  42.7 13.9 %convolution_bitcast_fusion = f32[2,128,128,128]{3,2,1,0:T(8,128)S(1)} fusion(f32[1,32,2,128]{3,1,0,2:T(8,128)S(1)} %get-tuple-element.32, f32[1,32,2,128]{3,1,0,2:T(8,128)S(1)} %get-tuple-element.31, f32[2,128,32,128]{3,2,1,0:T(8,128)S(1)} %bitcast.87), kind=kOutput, calls=%fused_computation.20 | convolution fusion | flops 3221241856 | bytes 21037056 | tf_op jit(solution)/shard_map/sfab,satd->tfdb/dot_general | solution.py:66
  56.6 7.0 %multiply_add_fusion = (f32[1,128,128,128]{3,2,1,0:T(8,128)}, f32[1,128,128,128]{3,2,1,0:T(8,128)}) fusion(f32[2,128,128,128]{3,2,1,0:T(8,128)S(1)} %convolution_bitcast_fusion, f32[128,128]{1,0:T(8,128)S(1)} %get-tuple-element.35, f32[128,128]{1,0:T(8,128)S(1)} %get-tuple-element.36), kind=kLoop, calls=%fused_computation.19 | loop fusion | flops 12582912 | bytes 33685504 | tf_op jit(solution)/shard_map/add | solution.py:67
  63.6 18.1 %fusion.49 = f32[2,128,32,128]{3,2,1,0:T(8,128)S(1)} fusion(f32[1,128,2,32]{1,3,0,2:T(8,128)S(1)} %get-tuple-element.30, f32[1,128,2,32]{1,3,0,2:T(8,128)S(1)} %get-tuple-element.29, f32[1,128,128,128]{3,2,1,0:T(8,128)} %get-tuple-element.7, f32[1,128,128,128]{3,2,1,0:T(8,128)} %get-tuple-element.6), kind=kOutput, calls=%fused_computation.82 | convolution fusion | flops 3225436160 | bytes 21037056 | tf_op jit(solution)/shard_map/tfdb,tbuc->ufcd/dot_general | solution.py:70
  81.7 0.6 fusion.86
  82.3 1.8 %add.161 = f32[32,4,4096]{2,1,0:T(4,128)} reshape(f32[1,128,32,128]{3,2,1,0:T(8,128)S(1)} %get-tuple-element.5) | data formatting | bytes 4194304 | tf_op jit(solution)/shard_map/add | solution.py:87
  84.0 2.9 %reduce_sum.42 = f32[32,4096]{1,0:T(8,128)S(1)} reduce(f32[32,4,4096]{2,1,0:T(4,128)} %add.161, f32[]{:T(128)} %constant.56.clone.1), dimensions={1}, to_apply=%region_0.1 | reduce | flops 393216 | bytes 2621444 | tf_op jit(solution)/shard_map/reduce_sum | solution.py:99
  86.9 0.1 copy.46
  87.0 0.1 broadcast_in_dim.4
  87.1 0.5 convolution_bitcast_fusion.1
  87.6 0.2 fusion.53
  87.8 1.1 copy.33
  88.9 9.4 %all-to-all-start = ((f32[32,32,128]{2,0,1:T(8,128)}), f32[32,32,128]{2,0,1:T(8,128)S(1)}, u32[]{:S(2)}, u32[]{:S(2)}) async-start(f32[32,32,128]{2,0,1:T(8,128)} %copy.33), calls=%async_computation | async-start | bytes 1048576 | tf_op jit(solution)/shard_map/all_to_all | solution.py:102
  98.3 11.4 %all-to-all-done = f32[32,32,128]{2,0,1:T(8,128)S(1)} async-done(((f32[32,32,128]{2,0,1:T(8,128)}), f32[32,32,128]{2,0,1:T(8,128)S(1)}, u32[]{:S(2)}, u32[]{:S(2)}) %all-to-all-start) | async-done | bytes 524320 | tf_op jit(solution)/shard_map/all_to_all | solution.py:102
  109.8 1.9 %broadcast_in_dim.5 = f32[32,1,8192]{2,1,0:T(1,128)} broadcast(f32[8192]{0:T(1024)S(1)} %pad_maximum_fusion.2), dimensions={2} | broadcast | bytes 1081344 | tf_op jit(solution)/shard_map/broadcast_in_dim | solution.py:20
  111.7 4.0 %all-to-all-start.1 = ((f32[32,1,8192]{2,1,0:T(1,128)}), f32[32,1,8192]{2,1,0:T(1,128)S(1)}, u32[]{:S(2)}, u32[]{:S(2)}) async-start(f32[32,1,8192]{2,1,0:T(1,128)} %broadcast_in_dim.5), calls=%async_computation.1 | async-start | bytes 2097152 | tf_op jit(solution)/shard_map/all_to_all | solution.py:19
  115.7 0.1 broadcast_bitcast_fusion
  115.7 17.1 %all-to-all-done.1 = f32[32,1,8192]{2,1,0:T(1,128)S(1)} async-done(((f32[32,1,8192]{2,1,0:T(1,128)}), f32[32,1,8192]{2,1,0:T(1,128)S(1)}, u32[]{:S(2)}, u32[]{:S(2)}) %all-to-all-start.1) | async-done | bytes 1048608 | tf_op jit(solution)/shard_map/all_to_all | solution.py:19
  132.8 0.7 reduce_sum.48
  133.5 0.7 multiply_reduce_fusion.1
  134.2 1.2 multiply_divide_fusion
  135.5 0.8 copy.58
  (3 shorter events, 0.0 us)
Async XLA Ops:
  1.7 10.7 %collective-permute-start = (f32[2,15,4096]{2,1,0:T(8,128)S(1)}, f32[2,15,4096]{2,1,0:T(8,128)S(1)}, u32[]{:S(2)}, u32[]{:S(2)}) collective-permute-start(f32[2,15,4096]{2,1,0:T(8,128)S(1)} %slice.122), channel_id=1, source_target_pairs={{0,1},{1,2},{2,3},{3,4},{4,5},{5,6},{6,7},{7,8},{8,9},{9,10},{10,1... | collective-permute-start | bytes 1474568 | tf_op jit(solution)/shard_map/ppermute | solution.py:14
  88.9 20.8 %all-to-all-start = ((f32[32,32,128]{2,0,1:T(8,128)}), f32[32,32,128]{2,0,1:T(8,128)S(1)}, u32[]{:S(2)}, u32[]{:S(2)}) async-start(f32[32,32,128]{2,0,1:T(8,128)} %copy.33), calls=%async_computation | async-start | bytes 1048576 | tf_op jit(solution)/shard_map/all_to_all | solution.py:102
  111.7 21.1 %all-to-all-start.1 = ((f32[32,1,8192]{2,1,0:T(1,128)}), f32[32,1,8192]{2,1,0:T(1,128)S(1)}, u32[]{:S(2)}, u32[]{:S(2)}) async-start(f32[32,1,8192]{2,1,0:T(1,128)} %broadcast_in_dim.5), calls=%async_computation.1 | async-start | bytes 2097152 | tf_op jit(solution)/shard_map/all_to_all | solution.py:19
where the time goes:
time: 137 us; the launch traced here: 136 us
  other arithmetic  44.7 us (33%)
  matrix products  32.5 us (24%)
  waiting for transfers between devices  30 us (22%)
  starting transfers between devices  18 us (13%)
  local copies, waits for them, and re-layouts  10.3 us (8%)
    add x1, other arithmetic, body(): filtered + taps[offset][None, None, :] * padded[:, begin:begin + frames, :]  29.5 us
    dot_general x1, matrix products, transform(): jnp.einsum('tfdb,tbuc->ufcd', twisted, inner_table, precision=lax.Precisi...  18.1 us
    all_to_all x1, waiting for transfers between devices, from_everyone(): lax.all_to_all(jnp.broadcast_to(value[None], (count, *value.shape)), axis...  17.1 us
    dot_general x1, matrix products, transform(): jnp.einsum('sfab,satd->tfdb', shaped, outer_table, precision=lax.Precisio...  13.9 us
    all_to_all x1, waiting for transfers between devices, body(): lax.all_to_all(local_dynamic, 'tm', split_axis=1, concat_axis=0, tiled=True)  11.4 us
    all_to_all x1, starting transfers between devices, body(): lax.all_to_all(local_dynamic, 'tm', split_axis=1, concat_axis=0, tiled=True)  9.4 us
    add x1, other arithmetic, transform(): twisted_real = sectioned[0] * twist_cos + sectioned[1] * twist_sin  7.04 us
    ppermute x1, starting transfers between devices, from_behind(): return lax.ppermute(value, axis, pairs)  4.58 us
  transfers between devices with their start and end apart: 3, of which 3 were waited for; matrix products, arithmetic and copies ran while one was open for 3% of the time, Pallas kernels for 0%

commit v1 on v0

v1 whole, which is shorter than its diff:
```python
import functools

import jax
import jax.numpy as jnp
import ml_dtypes
import numpy as np
from jax import lax
from jax.experimental import pallas as pl
from jax.experimental.pallas import tpu as pltpu
from jax.sharding import PartitionSpec as P

J, L = 32, 128
TAPS = 16
CHUNK = 16
ROWS = CHUNK // 4
F32, BF16 = jnp.float32, jnp.bfloat16
MESH = pl.DeviceIdType.MESH


def split_table(table):
    high = table.astype(ml_dtypes.bfloat16)
    low = (table - high.astype(np.float64)).astype(ml_dtypes.bfloat16)
    return high, low


def complex_table(turns, steps):
    angle = 2.0 * np.pi * (turns % steps) / steps
    cosine, sine = np.cos(angle), np.sin(angle)
    return cosine, sine


def tables():
    q, j = np.arange(J)[:, None], np.arange(J)[None, :]
    cosine, sine = complex_table(q * j, J)
    outer = np.block([[cosine, sine], [-sine, cosine]])
    high, low = split_table(outer)
    outer_table = np.concatenate([high, high, low], 1)
    cosine, sine = complex_table(q * np.arange(L)[None, :], J * L)
    twist = np.stack([cosine, sine]).astype(np.float32)
    a, m = np.arange(L)[:, None], np.arange(L)[None, :]
    cosine, sine = complex_table(a * m, L)
    inner = np.block([[cosine, -sine], [sine, cosine]])
    return outer_table, twist, np.stack(split_table(inner))


def split(value):
    high = value.astype(BF16)
    low = (value - high.astype(F32)).astype(BF16)
    return high, low


def dot(a, b):
    return jnp.dot(a, b, preferred_element_type=F32)


def exchange(rows):
    lane = lax.broadcasted_iota(jnp.int32, rows[0].shape, 1)
    rows = list(rows)
    for bit in (2, 1):
        upper = (lane & bit) != 0
        for a in range(4):
            if a & bit:
                continue
            x, y = rows[a], rows[a + bit]
            rows[a] = jnp.where(upper, pltpu.roll(y, bit, 1), x)
            rows[a + bit] = jnp.where(upper, y, pltpu.roll(x, L - bit, 1))
    return rows


def owners_first(rows):
    return jnp.concatenate(exchange(rows), axis=0).T


def kernel(
    groups, frames,
    volt, taps, mask, outer, twist, inner,
    dyn, kurt, spec,
    vbuf, ybuf, tbuf, mbuf, moments, got,
    load_sem, halo_send, halo_recv, row_send, row_recv, mom_send, mom_recv,
):
    me = lax.axis_index("tm")
    chunks = frames // CHUNK
    blocks = frames // 8

    def load(piece, first, count):
        return pltpu.make_async_copy(
            volt.at[:, pl.ds(first, count)], vbuf.at[:, pl.ds(first + 2, count)], load_sem.at[piece]
        )

    load(0, blocks - 2, 2).start()
    load(1, 0, 4).start()
    for c in range(2, chunks - 1):
        load(c, 2 * c, 2).start()

    barrier = pltpu.get_barrier_semaphore()
    for d in range(1, groups):
        pl.semaphore_signal(barrier, 1, device_id={"tm": lax.rem(me + d, groups)}, device_id_type=MESH)

    def fir_part(c, s, jb, slot):
        t = [taps[pl.ds((k // 8) * 256 + jb * 64 + k % 8, 8, stride=8), :] for k in range(TAPS)]
        x = []
        for g in range(1, 2 * CHUNK):
            ref = vbuf.at[s, 2 * c + g // 8]
            x.append(ref[pl.ds(jb * 64 + g % 8, 8, stride=8), :])
        for f in range(CHUNK):
            total = t[0] * x[f + TAPS - 1]
            for k in range(1, TAPS):
                total = total + t[k] * x[f + TAPS - 1 - k]
            ybuf[slot, f, pl.ds(s * J + jb * 8, 8), :] = total

    def dft_part(quad, slot):
        cosine, sine = twist[0], twist[1]
        z = []
        for pair in range(2):
            f = quad * 4 + pair * 2
            y = jnp.concatenate([ybuf[slot, f], ybuf[slot, f + 1]], axis=1)
            high, low = split(y)
            o = dot(outer[...], jnp.concatenate([high, low, high], axis=0))
            for h in range(2):
                re, im = o[:J, h * L:(h + 1) * L], o[J:, h * L:(h + 1) * L]
                z.append(jnp.concatenate([re * cosine + im * sine, im * cosine - re * sine], axis=1))
        high, low = split(jnp.concatenate(z, axis=0))
        x = dot(high, inner[0]) + dot(low, inner[0]) + dot(high, inner[1])
        power = x[:, :L] * x[:, :L] + x[:, L:] * x[:, L:]
        p = [power[f * J:(f + 1) * J] for f in range(4)]
        row = (p[0] + p[1]) + (p[2] + p[3])
        moments[0] += row
        moments[1] += (p[0] * p[0] + p[1] * p[1]) + (p[2] * p[2] + p[3] * p[3])
        return row

    def send(src, dst, dest, send_sem, recv_sem):
        return pltpu.make_async_remote_copy(
            src, dst, send_sem, recv_sem, device_id={"tm": dest}, device_id_type=MESH
        )

    def finish_rows(c, rows):
        clean = mask[...]
        scaled = []
        for row in rows:
            part = jnp.sum(row, axis=0, keepdims=True) * clean
            total = jnp.sum(part, axis=1, keepdims=True)
            moments[2, pl.ds(0, 1), :] += part
            scaled.append(row * (clean * float(J * L)) * (1.0 / total))
        tbuf[c] = owners_first(scaled).reshape(groups, ROWS, L)
        for d in range(1, groups):
            dest = lax.rem(me + d, groups)
            send(tbuf.at[c, dest], dyn.at[me, c], dest, row_send, row_recv).start()
        dyn[me, c] = tbuf[c, me]

    moments[...] = jnp.zeros_like(moments)

    load(1, 0, 4).wait()
    for s in range(2):
        for jb in range(4):
            fir_part(1, s, jb, 1)
    load(0, blocks - 2, 2).wait()
    pl.semaphore_wait(barrier, groups - 1)

    def halo(dest):
        return send(
            vbuf.at[:, pl.ds(blocks, 2)], vbuf.at[:, pl.ds(0, 2)], dest, halo_send, halo_recv
        )

    following = lax.rem(me + 1, groups)

    @pl.when(me < groups - 1)
    def _():
        halo(following).start()

    @pl.loop(1, chunks - 1)
    def _(c):
        @pl.when(c < chunks - 2)
        def _():
            load(c + 1, 2 * (c + 1), 2).wait()

        rows = []
        for part in range(4):
            fir_part(c + 1, part // 2, part % 2 * 2, lax.rem(c + 1, 2))
            fir_part(c + 1, part // 2, part % 2 * 2 + 1, lax.rem(c + 1, 2))
            rows.append(dft_part(part, lax.rem(c, 2)))
        finish_rows(c, rows)

    finish_rows(chunks - 1, [dft_part(part, (chunks - 1) % 2) for part in range(4)])

    @pl.when(me > 0)
    def _():
        halo(following).wait_recv()

    @pl.when(me == 0)
    def _():
        vbuf[:, pl.ds(0, 2)] = jnp.zeros((2, 2, 256, L), F32)

    for s in range(2):
        for jb in range(4):
            fir_part(0, s, jb, 0)
    finish_rows(0, [dft_part(part, 0) for part in range(4)])

    local = jnp.sum(moments[2, pl.ds(0, 1), :], axis=1, keepdims=True)
    last = [moments[0], moments[1], jnp.broadcast_to(local, (J, L)), jnp.zeros((J, L), F32)]
    mbuf[...] = owners_first(last).reshape(groups, 4, L)
    for d in range(1, groups):
        dest = lax.rem(me + d, groups)
        send(mbuf.at[dest], got.at[me], dest, mom_send, mom_recv).start()
    got[me] = mbuf[me]

    everyone = pl.ds(0, groups - 1)
    send(mbuf.at[everyone], got.at[everyone], following, mom_send, mom_recv).wait_recv()
    sums = jnp.sum(got[...], axis=0)
    first, second, group = sums[0:1], sums[1:2], sums[2:3]
    count = float(frames * groups)
    kurt[...] = (count + 1.0) / (count - 1.0) * (count * second / (first * first) - 1.0)
    lane = lax.broadcasted_iota(jnp.int32, (1, L), 1)
    mine = jnp.sum(jnp.where(lane == 4 * me, mask[...], 0.0), axis=1, keepdims=True)
    spec[...] = float(J * L) * mine * first / group

    send(dyn.at[everyone], dyn.at[everyone], following, row_send, row_recv).wait()
    send(mbuf.at[everyone], got.at[everyone], following, mom_send, mom_recv).wait_send()

    @pl.when(me < groups - 1)
    def _():
        halo(following).wait_send()


def body(groups, voltages, taps, flags):
    frames = voltages.shape[1]
    chunks = frames // CHUNK
    volt = voltages.reshape(2, frames // 8, 8, J, L).transpose(0, 1, 3, 2, 4).reshape(2, frames // 8, 8 * J, L)
    tap = taps.reshape(TAPS // 8, 8, J, L).transpose(0, 2, 1, 3).reshape(TAPS * J, L)
    mask = jnp.broadcast_to((1 - flags).astype(F32)[:, None], (groups, 4)).reshape(1, L)
    outer, twist, inner = tables()
    vmem = pl.BlockSpec(memory_space=pltpu.VMEM)
    dyn, kurt, spec = pl.pallas_call(
        functools.partial(kernel, groups, frames),
        out_shape=(
            jax.ShapeDtypeStruct((groups, chunks, ROWS, L), F32),
            jax.ShapeDtypeStruct((1, L), F32),
            jax.ShapeDtypeStruct((1, L), F32),
        ),
        in_specs=[pl.BlockSpec(memory_space=pl.ANY)] + [vmem] * 5,
        out_specs=(vmem, vmem, vmem),
        scratch_shapes=[
            pltpu.VMEM((2, frames // 8 + 2, 8 * J, L), F32),
            pltpu.VMEM((2, CHUNK, 2 * J, L), F32),
            pltpu.VMEM((chunks, groups, ROWS, L), F32),
            pltpu.VMEM((groups, 4, L), F32),
            pltpu.VMEM((3, J, L), F32),
            pltpu.VMEM((groups, 4, L), F32),
            pltpu.SemaphoreType.DMA((chunks,)),
        ] + [pltpu.SemaphoreType.DMA] * 6,
        compiler_params=pltpu.CompilerParams(
            collective_id=0, has_side_effects=True, vmem_limit_bytes=40 * 1024 * 1024
        ),
    )(volt, tap, mask, jnp.asarray(outer), jnp.asarray(twist), jnp.asarray(inner))
    return dyn.reshape(groups * frames // 4, L), kurt.reshape(L), spec.reshape(L)


def solution(mesh):
    placed = (P(None, ("stream", "tm"), None), P(), P("stream"))
    return jax.shard_map(
        functools.partial(body, mesh.shape["tm"]),
        mesh=mesh,
        in_specs=placed,
        out_specs=(P("stream", "tm"), P(("stream", "tm")), P(("stream", "tm"))),
        check_vma=False,
    )
```

time: 137 us -> 37 us (0.27)
  other arithmetic: 44.7 us -> 0.66 us
  matrix products: 32.5 us -> 0 us
  waiting for transfers between devices: 30 us -> 0 us
  Pallas kernels: 0 us -> 27.8 us
  starting transfers between devices: 18 us -> 0 us
  local copies, waits for them, and re-layouts: 10.3 us -> 7.59 us
    add x2 -> x0, other arithmetic: 36.5 us -> none  [the longest x1 29.5 us: body(): filtered + taps[offset][None, None, :] * padded[:, begin:begin + frames, :]]
    dot_general x3 -> x0, matrix products: 32.5 us -> none  [the longest x1 18.1 us: transform(): jnp.einsum('tfdb,tbuc->ufcd', twisted, inner_table, precision=lax.Precisi...]
    all_to_all x2 -> x0, waiting for transfers between devices: 28.5 us -> none  [the longest x1 17.1 us: from_everyone(): lax.all_to_all(jnp.broadcast_to(value[None], (count, *value.shape)), axis...]
    pallas_call x0 -> x1, Pallas kernels: none -> 27.8 us  [body(): pl.pallas_call(functools.partial(kernel, groups, frames), out_shape=(jax....]
    all_to_all x2 -> x0, starting transfers between devices: 13.4 us -> none  [the longest x1 9.4 us: body(): lax.all_to_all(local_dynamic, 'tm', split_axis=1, concat_axis=0, tiled=True)]
    unnamed x3 -> x13, local copies, waits for them, and re-layouts: 1.64 us -> 7.42 us
    ppermute x1 -> x0, starting transfers between devices: 4.58 us -> none  [from_behind(): return lax.ppermute(value, axis, pairs)]
    reduce_sum x3 -> x0, other arithmetic: 4.14 us -> none  [the longest x1 2.88 us: body(): jnp.sum(channel_powers.reshape(frames // SUMMED, SUMMED, channel_list), a...]
  transfers between devices with their start and end apart: 3 -> 0, of which waited for: 3 -> 0; matrix products, arithmetic and copies ran while one was open for 3% -> 0% of each run, Pallas kernels for 0% -> 0%
where the time goes in v1:
time: 37 us; the launch traced here: 36.7 us
  Pallas kernels  27.8 us (75%)
  local copies, waits for them, and re-layouts  7.59 us (21%)
  other arithmetic  0.66 us (2%)
  between operations  0.66 us (2%)
    pallas_call x1, Pallas kernels, body(): pl.pallas_call(functools.partial(kernel, groups, frames), out_shape=(jax....  27.8 us
    unnamed x13, local copies, waits for them, and re-layouts  7.42 us

profile of v1, /device:TPU:1, one launch (start us, length us, event | category | flops | bytes accessed | tf_op | source)
XLA Modules:
  0.0 36.7 jit_solution(7433451982322377550)
XLA Ops:
  0.6 0.7 %subtract_convert_fusion = f32[32]{0:T(128)S(1)} fusion(s32[32]{0:T(128)} %param.8), kind=kLoop, calls=%fused_computation | loop fusion | flops 64 | bytes 256 | tf_op jit(solution)/shard_map/convert_element_type | solution.py:229
  1.3 0.1 broadcast_in_dim.2
  1.4 0.1 reshape.35.mask
  1.5 0.0 copy-start
  1.5 2.2 %copy-done = f32[2,128,4096]{2,1,0:T(8,128)S(1)} copy-done((f32[2,128,4096]{2,1,0:T(8,128)S(1)}, f32[2,128,4096]{2,1,0:T(8,128)}, u32[]{:S(2)}) %copy-start) | copy-done | bytes 4194328
  3.7 0.0 copy-start.1
  3.7 0.9 %copy-done.1 = f32[16,4096]{1,0:T(8,128)S(1)} copy-done((f32[16,4096]{1,0:T(8,128)S(1)}, f32[16,4096]{1,0:T(8,128)}, u32[]{:S(2)}) %copy-start.1) | copy-done | bytes 262168
  4.6 0.0 copy-start.2
  4.6 0.9 %copy-done.2 = bf16[2,256,256]{2,1,0:T(8,128)(2,1)S(1)} copy-done((bf16[2,256,256]{2,1,0:T(8,128)(2,1)S(1)}, bf16[2,256,256]{2,1,0:T(8,128)(2,1)}, u32[]{:S(2)}) %copy-start.2) | copy-done | bytes 262168
  5.6 0.0 copy-start.3
  5.6 0.8 %copy-done.3 = f32[2,32,128]{2,1,0:T(8,128)S(1)} copy-done((f32[2,32,128]{2,1,0:T(8,128)S(1)}, f32[2,32,128]{2,1,0:T(8,128)}, u32[]{:S(2)}) %copy-start.3) | copy-done | bytes 32792
  6.3 0.0 copy-start.4
  6.3 0.8 %copy-done.4 = bf16[64,192]{1,0:T(8,128)(2,1)S(1)} copy-done((bf16[64,192]{1,0:T(8,128)(2,1)S(1)}, bf16[64,192]{1,0:T(8,128)(2,1)}, u32[]{:S(2)}) %copy-start.4) | copy-done | bytes 24600
  7.1 27.8 %shard_map.85 = (f32[32,8,4,128]{3,2,1,0:T(4,128)S(1)}, f32[1,128]{1,0:T(1,128)S(1)}, f32[1,128]{1,0:T(1,128)S(1)}) custom-call(f32[2,16,256,128]{3,2,1,0:T(8,128)S(1)} %bitcast.13, f32[512,128]{1,0:T(8,128)S(1)} %bitcast.15, f32[1,128]{1,0:T(1,128)S(1)} %reshape.35.mask, bf16[64,192]{1,0:T(8,128)(2,1)S(1)} %copy-done.4, f32[2,32,128]{2,1,0:T(8,128)S(1)} %copy-done.3, ...), custom_call_target="tpu_custom_call" | custom-call | tf_op jit(solution)/shard_map/pallas_call | solution.py:232
  34.9 0.8 %copy.12 = f32[1024,128]{1,0:T(8,128)} copy(f32[1024,128]{1,0:T(8,128)S(1)} %bitcast.14) | data formatting | bytes 1048576
  35.7 0.5 %copy.13 = f32[128]{0:T(128)} copy(f32[128]{0:T(128)S(1)} %bitcast.17) | data formatting | bytes 1024
  36.2 0.5 %copy.14 = f32[128]{0:T(128)} copy(f32[128]{0:T(128)S(1)} %bitcast.16) | data formatting | bytes 1024
Async XLA Ops:
  1.5 2.2 %copy-start = (f32[2,128,4096]{2,1,0:T(8,128)S(1)}, f32[2,128,4096]{2,1,0:T(8,128)}, u32[]{:S(2)}) copy-start(f32[2,128,4096]{2,1,0:T(8,128)} %param.6) | copy-start | bytes 12582916
  3.7 0.9 %copy-start.1 = (f32[16,4096]{1,0:T(8,128)S(1)}, f32[16,4096]{1,0:T(8,128)}, u32[]{:S(2)}) copy-start(f32[16,4096]{1,0:T(8,128)} %param.7) | copy-start | bytes 786436
  4.6 0.9 %copy-start.2 = (bf16[2,256,256]{2,1,0:T(8,128)(2,1)S(1)}, bf16[2,256,256]{2,1,0:T(8,128)(2,1)}, u32[]{:S(2)}) copy-start(bf16[2,256,256]{2,1,0:T(8,128)(2,1)} %constant.10.clone.inner) | copy-start | bytes 786436
  5.6 0.8 %copy-start.3 = (f32[2,32,128]{2,1,0:T(8,128)S(1)}, f32[2,32,128]{2,1,0:T(8,128)}, u32[]{:S(2)}) copy-start(f32[2,32,128]{2,1,0:T(8,128)} %constant.9.clone.twist) | copy-start | bytes 98308
  6.3 0.8 %copy-start.4 = (bf16[64,192]{1,0:T(8,128)(2,1)S(1)}, bf16[64,192]{1,0:T(8,128)(2,1)}, u32[]{:S(2)}) copy-start(bf16[64,192]{1,0:T(8,128)(2,1)} %constant.8.clone.outer) | copy-start | bytes 73732

commit v2 on v1

v2 whole, which is shorter than its diff:
```python
import functools

import jax
import jax.numpy as jnp
import ml_dtypes
import numpy as np
from jax import lax
from jax.experimental import pallas as pl
from jax.experimental.pallas import tpu as pltpu
from jax.sharding import PartitionSpec as P

J, L = 32, 128
TAPS = 16
CHUNK = 32
F32, BF16 = jnp.float32, jnp.bfloat16
MESH = pl.DeviceIdType.MESH


def split_table(table):
    high = table.astype(ml_dtypes.bfloat16)
    low = (table - high.astype(np.float64)).astype(ml_dtypes.bfloat16)
    return high, low


def complex_table(turns, steps):
    angle = 2.0 * np.pi * (turns % steps) / steps
    cosine, sine = np.cos(angle), np.sin(angle)
    return cosine, sine


def tables():
    q, j = np.arange(J)[:, None], np.arange(J)[None, :]
    cosine, sine = complex_table(q * j, J)
    outer = np.block([[cosine, sine], [-sine, cosine]])
    high, low = split_table(outer)
    outer_table = np.concatenate([high, high, low], 1)
    cosine, sine = complex_table(q * np.arange(L)[None, :], J * L)
    twist = np.stack([cosine, sine]).astype(np.float32)
    a, m = np.arange(L)[:, None], np.arange(L)[None, :]
    cosine, sine = complex_table(a * m, L)
    inner = np.block([[cosine, -sine], [sine, cosine]])
    return outer_table, twist, np.stack(split_table(inner))


def split(value):
    high = value.astype(BF16)
    low = (value - high.astype(F32)).astype(BF16)
    return high, low


def dot(a, b):
    return jnp.dot(a, b, preferred_element_type=F32)


def exchange(rows):
    lane = lax.broadcasted_iota(jnp.int32, rows[0].shape, 1)
    rows = list(rows)
    for bit in (2, 1):
        upper = (lane & bit) != 0
        for a in range(4):
            if a & bit:
                continue
            x, y = rows[a], rows[a + bit]
            rows[a] = jnp.where(upper, pltpu.roll(y, bit, 1), x)
            rows[a + bit] = jnp.where(upper, y, pltpu.roll(x, L - bit, 1))
    return rows


def owners_first(rows):
    return jnp.concatenate(exchange(rows), axis=0).T


def kernel(
    groups, frames,
    volt, taps_in, flags_in, outer_in, twist_in, inner_in,
    dyn, kurt, spec,
    vbuf, taps, flags, outer, twist, inner, ybuf, zbuf, held, tbuf, mbuf, moments, got,
    load_sem, halo_send, halo_recv, row_send, row_recv, mom_send, mom_recv,
):
    me = lax.axis_index("tm")
    chunks = frames // CHUNK
    blocks = frames // 8
    span = CHUNK // 8

    def load(piece, part, first, count):
        return pltpu.make_async_copy(
            volt.at[part, pl.ds(first, count)], vbuf.at[part, pl.ds(first + 2, count)], load_sem.at[piece]
        )

    both = pl.ds(0, 2)
    loads = [
        pltpu.make_async_copy(taps_in, taps, load_sem.at[0]),
        load(1, 0, span - 2, span + 2),
        load(2, 1, span - 2, span + 2),
        load(3, both, blocks - 2, 2),
        pltpu.make_async_copy(outer_in, outer, load_sem.at[4]),
        pltpu.make_async_copy(twist_in, twist, load_sem.at[5]),
        pltpu.make_async_copy(inner_in, inner, load_sem.at[6]),
        pltpu.make_async_copy(flags_in, flags, load_sem.at[7]),
        load(8, both, 2 * span, blocks - 2 - 2 * span),
        load(9, both, 0, span - 2),
    ]
    for one in loads:
        one.start()

    barrier = pltpu.get_barrier_semaphore()
    for d in range(1, groups):
        pl.semaphore_signal(barrier, 1, device_id={"tm": lax.rem(me + d, groups)}, device_id_type=MESH)

    def fir(c, s):
        @pl.loop(0, J // 8)
        def _(jb):
            def tap(k):
                return taps[pl.ds(jb * 64 + ((k // 8) * 256 + k % 8), 8, stride=8), :]

            def sample(g):
                return vbuf.at[s, span * c + (g + 16) // 8][pl.ds(jb * 64 + (g + 16) % 8, 8, stride=8), :]

            half = TAPS // 2
            even_taps = [tap(2 * i) for i in range(half)]
            odd_taps = [tap(2 * i + 1) for i in range(half)]
            sum_taps = [a + b for a, b in zip(even_taps, odd_taps)]

            def run(h, x):
                total = h[0] * x[half - 1]
                for i in range(1, half):
                    total = total + h[i] * x[half - 1 - i]
                return total

            even = [sample(2 * n) for n in range(1 - half, 0)]
            odd = [sample(2 * n + 1) for n in range(-half, 0)]
            both_x = [a + b for a, b in zip(even, odd[1:])]
            before = run(odd_taps, odd)
            for n in range(CHUNK // 2):
                even, odd = (even + [sample(2 * n)])[-half:], odd[1:] + [sample(2 * n + 1)]
                both_x = (both_x + [even[-1] + odd[-1]])[-half:]
                a, b, ab = run(even_taps, even), run(odd_taps, odd), run(sum_taps, both_x)
                place = pl.ds(pl.multiple_of(s * J + jb * 8, 8), 8)
                ybuf[2 * n, place, :] = a + before
                ybuf[2 * n + 1, place, :] = ab - (a + b)
                before = b

    def first_stage(part):
        cosine, sine = twist[0], twist[1]
        for pair in range(4):
            f = part * 8 + pair * 2
            y = jnp.concatenate([ybuf[f], ybuf[f + 1]], axis=1)
            high, low = split(y)
            o = dot(outer[...], jnp.concatenate([high, low, high], axis=0))
            for h in range(2):
                re, im = o[:J, h * L:(h + 1) * L], o[J:, h * L:(h + 1) * L]
                z = jnp.concatenate([re * cosine + im * sine, im * cosine - re * sine], axis=1)
                place = pl.ds((pair * 2 + h) * J, J)
                zbuf[part, 0, place, :], zbuf[part, 1, place, :] = split(z)

    def second_stage(part):
        high, low = zbuf[part, 0], zbuf[part, 1]
        x = dot(high, inner[0]) + dot(low, inner[0]) + dot(high, inner[1])
        power = x[:, :L] * x[:, :L] + x[:, L:] * x[:, L:]
        for r in range(2):
            p = [power[(4 * r + f) * J:(4 * r + f + 1) * J] for f in range(4)]
            row = (p[0] + p[1]) + (p[2] + p[3])
            moments[0] += row
            moments[1] += (p[0] * p[0] + p[1] * p[1]) + (p[2] * p[2] + p[3] * p[3])
            held[part * 2 + r] = row

    def send(src, dst, dest, send_sem, recv_sem):
        return pltpu.make_async_remote_copy(
            src, dst, send_sem, recv_sem, device_id={"tm": dest}, device_id_type=MESH
        )

    def clean_lanes():
        block = lax.broadcasted_iota(jnp.int32, (groups, L), 0)
        lane = lax.broadcasted_iota(jnp.int32, (groups, L), 1)
        spread = jnp.where(lane // 4 == block, 1.0, 0.0)
        clean = jnp.broadcast_to(1.0 - flags[...].astype(F32), (8, groups))
        return dot(clean.astype(BF16), spread.astype(BF16))[0:1]

    def finish_rows(c, side):
        clean = moments[2, pl.ds(8, 1), :]
        scaled = []
        for a in range(4):
            row = held[side * 4 + a]
            part = jnp.sum(row, axis=0, keepdims=True) * clean
            total = jnp.sum(part, axis=1, keepdims=True)
            moments[2, pl.ds(0, 1), :] += part
            scaled.append(row * (clean * float(J * L)) * (1.0 / total))
        tbuf[c, side] = owners_first(scaled).reshape(groups, 4, L)

    def send_rows(c):
        for d in range(1, groups):
            dest = lax.rem(me + d, groups)
            send(tbuf.at[c, both, dest], dyn.at[me, c], dest, row_send, row_recv).start()
        dyn[me, c] = tbuf[c, both, me]

    def halo(dest):
        return send(
            vbuf.at[:, pl.ds(blocks, 2)], vbuf.at[:, pl.ds(0, 2)], dest, halo_send, halo_recv
        )

    following = lax.rem(me + 1, groups)
    moments[...] = jnp.zeros_like(moments)

    loads[0].wait()
    loads[1].wait()
    fir(1, 0)
    loads[2].wait()
    fir(1, 1)
    loads[3].wait()
    pl.semaphore_wait(barrier, groups - 1)

    @pl.when(me < groups - 1)
    def _():
        halo(following).start()

    for piece in range(4, 10):
        loads[piece].wait()
    moments[2, pl.ds(8, 1), :] = clean_lanes()

    def spectra(c, earlier):
        first_stage(0)
        if earlier is not None:
            finish_rows(earlier, 1)
        first_stage(1)
        second_stage(0)
        first_stage(2)
        second_stage(1)
        if earlier is not None:
            send_rows(earlier)
        finish_rows(c, 0)
        first_stage(3)
        second_stage(2)
        second_stage(3)

    spectra(1, None)

    @pl.loop(2, chunks + 1)
    def _(i):
        c = lax.rem(i, chunks)

        @pl.when(i == chunks)
        def _():
            @pl.when(me > 0)
            def _():
                halo(following).wait_recv()

            @pl.when(me == 0)
            def _():
                vbuf[:, pl.ds(0, 2)] = jnp.zeros((2, 2, 8 * J, L), F32)

        fir(c, 0)
        fir(c, 1)
        spectra(c, i - 1)

    finish_rows(0, 1)
    send_rows(0)

    local = jnp.sum(moments[2, pl.ds(0, 1), :], axis=1, keepdims=True)
    last = [moments[0], moments[1], jnp.broadcast_to(local, (J, L)), jnp.zeros((J, L), F32)]
    mbuf[...] = owners_first(last).reshape(groups, 4, L)
    for d in range(1, groups):
        dest = lax.rem(me + d, groups)
        send(mbuf.at[dest], got.at[me], dest, mom_send, mom_recv).start()
    got[me] = mbuf[me]

    everyone = pl.ds(0, groups - 1)
    send(mbuf.at[everyone], got.at[everyone], following, mom_send, mom_recv).wait_recv()
    sums = jnp.sum(got[...], axis=0)
    first, second, group = sums[0:1], sums[1:2], sums[2:3]
    count = float(frames * groups)
    kurt[...] = (count + 1.0) / (count - 1.0) * (count * second / (first * first) - 1.0)
    lane = lax.broadcasted_iota(jnp.int32, (1, L), 1)
    mine = jnp.sum(jnp.where(lane == 4 * me, moments[2, pl.ds(8, 1), :], 0.0), axis=1, keepdims=True)
    spec[...] = float(J * L) * mine * first / group

    send(dyn.at[everyone], dyn.at[everyone], following, row_send, row_recv).wait()
    send(mbuf.at[everyone], got.at[everyone], following, mom_send, mom_recv).wait_send()

    @pl.when(me < groups - 1)
    def _():
        halo(following).wait_send()


def body(groups, voltages, taps, flags):
    frames = voltages.shape[1]
    chunks = frames // CHUNK
    volt = voltages.reshape(2, frames // 8, 8, J, L).transpose(0, 1, 3, 2, 4).reshape(2, frames // 8, 8 * J, L)
    tap = taps.reshape(TAPS // 8, 8, J, L).transpose(0, 2, 1, 3).reshape(TAPS * J, L)
    outer, twist, inner = tables()
    vmem = pl.BlockSpec(memory_space=pltpu.VMEM)
    dyn, kurt, spec = pl.pallas_call(
        functools.partial(kernel, groups, frames),
        out_shape=(
            jax.ShapeDtypeStruct((groups, chunks, CHUNK // 16, 4, L), F32),
            jax.ShapeDtypeStruct((1, L), F32),
            jax.ShapeDtypeStruct((1, L), F32),
        ),
        in_specs=[pl.BlockSpec(memory_space=pl.ANY)] * 6,
        out_specs=(vmem, vmem, vmem),
        scratch_shapes=[
            pltpu.VMEM((2, frames // 8 + 2, 8 * J, L), F32),
            pltpu.VMEM((TAPS * J, L), F32),
            pltpu.VMEM((1, groups), jnp.int32),
            pltpu.VMEM(outer.shape, BF16),
            pltpu.VMEM(twist.shape, F32),
            pltpu.VMEM(inner.shape, BF16),
            pltpu.VMEM((CHUNK, 2 * J, L), F32),
            pltpu.VMEM((CHUNK // 8, 2, 8 * J, 2 * L), BF16),
            pltpu.VMEM((CHUNK // 4, J, L), F32),
            pltpu.VMEM((chunks, CHUNK // 16, groups, 4, L), F32),
            pltpu.VMEM((groups, 4, L), F32),
            pltpu.VMEM((3, J, L), F32),
            pltpu.VMEM((groups, 4, L), F32),
            pltpu.SemaphoreType.DMA((10,)),
        ] + [pltpu.SemaphoreType.DMA] * 6,
        compiler_params=pltpu.CompilerParams(
            collective_id=0, has_side_effects=True, vmem_limit_bytes=63 * 1024 * 1024
        ),
    )(volt, tap, flags.reshape(1, groups), jnp.asarray(outer), jnp.asarray(twist), jnp.asarray(inner))
    return dyn.reshape(groups * frames // 4, L), kurt.reshape(L), spec.reshape(L)


def solution(mesh):
    placed = (P(None, ("stream", "tm"), None), P(), P("stream"))
    return jax.shard_map(
        functools.partial(body, mesh.shape["tm"]),
        mesh=mesh,
        in_specs=placed,
        out_specs=(P("stream", "tm"), P(("stream", "tm")), P(("stream", "tm"))),
        check_vma=False,
    )
```

time: 37 us -> 30.6 us (0.83)
  local copies, waits for them, and re-layouts: 7.59 us -> 4.15 us
  Pallas kernels: 27.8 us -> 25.6 us
  other arithmetic: 0.66 us -> 0 us
    unnamed x13 -> x3, local copies, waits for them, and re-layouts: 7.42 us -> 4.15 us
    pallas_call x1, Pallas kernels: 27.8 us -> 25.6 us  [body(): pl.pallas_call(functools.partial(kernel, groups, frames), out_shape=(jax....]
    convert_element_type x1 -> x0, other arithmetic: 0.66 us -> none  [body(): (1 - flags).astype(F32)[:, None]]
where the time goes in v2:
time: 30.6 us; the launch traced here: 30.4 us
  Pallas kernels  25.6 us (84%)
  local copies, waits for them, and re-layouts  4.15 us (14%)
  between operations  0.64 us (2%)
    pallas_call x1, Pallas kernels, body(): pl.pallas_call(functools.partial(kernel, groups, frames), out_shape=(jax....  25.6 us
    unnamed x3, local copies, waits for them, and re-layouts  4.15 us

profile of v2, /device:TPU:1, one launch (start us, length us, event | category | flops | bytes accessed | tf_op | source)
XLA Modules:
  0.0 30.4 jit_solution(6642474586224473146)
XLA Ops:
  0.6 25.6 %shard_map.85 = (f32[32,4,2,4,128]{4,3,2,1,0:T(4,128)}, f32[1,128]{1,0:T(1,128)}, f32[1,128]{1,0:T(1,128)}) custom-call(f32[2,16,256,128]{3,2,1,0:T(8,128)} %bitcast.14, f32[512,128]{1,0:T(8,128)} %bitcast.16, s32[1,32]{1,0:T(1,128)} %bitcast.17, bf16[64,192]{1,0:T(8,128)(2,1)} %constant.6.clone.outer_in, f32[2,32,128]{2,1,0:T(8,128)} %constant.7.clone.twist_in, ...), custom_call_target="tpu_custom_call" | custom-call | tf_op jit(solution)/shard_map/pallas_call | solution.py:291
  26.2 1.9 %copy.12 = f32[1024,128]{1,0:T(8,128)} copy(f32[1024,128]{1,0:T(8,128)} %bitcast.15) | data formatting | bytes 1048576
  28.1 1.1 %copy.13 = f32[128]{0:T(128)} copy(f32[128]{0:T(128)} %bitcast.19) | data formatting | bytes 1024
  29.2 1.2 %copy.14 = f32[128]{0:T(128)} copy(f32[128]{0:T(128)} %bitcast.18) | data formatting | bytes 1024

commit v3 on v2

v3 whole, which is shorter than its diff:
```python
import functools

import jax
import jax.numpy as jnp
import ml_dtypes
import numpy as np
from jax import lax
from jax.experimental import pallas as pl
from jax.experimental.pallas import tpu as pltpu
from jax.sharding import PartitionSpec as P

J, L = 32, 128
TAPS = 16
CHUNK = 32
FAR_FIRST = sorted(
    ((dz, dy) for dz in range(4) for dy in range(4)), key=lambda d: -(min(d[0], 4 - d[0]) + min(d[1], 4 - d[1]))
)
F32, BF16 = jnp.float32, jnp.bfloat16
MESH = pl.DeviceIdType.MESH


def split_table(table):
    high = table.astype(ml_dtypes.bfloat16)
    low = (table - high.astype(np.float64)).astype(ml_dtypes.bfloat16)
    return high, low


def complex_table(turns, steps):
    angle = 2.0 * np.pi * (turns % steps) / steps
    cosine, sine = np.cos(angle), np.sin(angle)
    return cosine, sine


def tables():
    q, j = np.arange(J)[:, None], np.arange(J)[None, :]
    cosine, sine = complex_table(q * j, J)
    outer = np.block([[cosine, sine], [-sine, cosine]])
    high, low = split_table(outer)
    outer_table = np.concatenate([high, high, low], 1)
    cosine, sine = complex_table(q * np.arange(L)[None, :], J * L)
    twist = np.stack([cosine, sine]).astype(np.float32)
    a, m = np.arange(L)[:, None], np.arange(L)[None, :]
    cosine, sine = complex_table(a * m, L)
    inner = np.block([[cosine, -sine], [sine, cosine]])
    return outer_table, twist, np.stack(split_table(inner))


def split(value):
    high = value.astype(BF16)
    low = (value - high.astype(F32)).astype(BF16)
    return high, low


def dot(a, b):
    return jnp.dot(a, b, preferred_element_type=F32)


def exchange(rows):
    lane = lax.broadcasted_iota(jnp.int32, rows[0].shape, 1)
    rows = list(rows)
    for bit in (2, 1):
        upper = (lane & bit) != 0
        for a in range(4):
            if a & bit:
                continue
            x, y = rows[a], rows[a + bit]
            rows[a] = jnp.where(upper, pltpu.roll(y, bit, 1), x)
            rows[a + bit] = jnp.where(upper, y, pltpu.roll(x, L - bit, 1))
    return rows


def owners_first(rows):
    return jnp.concatenate(exchange(rows), axis=0).T


def kernel(
    groups, frames,
    volt, taps_in, flags_in, outer_in, twist_in, inner_in,
    dyn, kurt, spec,
    vbuf, taps, flags, outer, twist, inner, half_taps, xbuf, ybuf, zbuf, held, wide, narrow, final, moments, got,
    load_sem, ready, halo_send, halo_recv, row_send, row_recv, fin_send, fin_recv,
):
    me = lax.axis_index("tm")
    blocks = frames // 8
    half = TAPS // 2
    both = pl.ds(0, 2)
    following, preceding = lax.rem(me + 1, groups), lax.rem(me + groups - 1, groups)

    def load(piece, part, first, count):
        return pltpu.make_async_copy(
            volt.at[part, pl.ds(first, count)], vbuf.at[part, pl.ds(first + 2, count)], load_sem.at[piece]
        )

    loads = [
        pltpu.make_async_copy(taps_in, taps, load_sem.at[0]),
        load(1, both, blocks - 2, 2),
        load(2, 0, 0, 6),
        load(3, 1, 0, 6),
        pltpu.make_async_copy(outer_in, outer, load_sem.at[4]),
        pltpu.make_async_copy(twist_in, twist, load_sem.at[5]),
        pltpu.make_async_copy(inner_in, inner, load_sem.at[6]),
        pltpu.make_async_copy(flags_in, flags, load_sem.at[7]),
        load(8, both, 6, 4),
        load(9, both, 10, 4),
    ]
    for one in loads:
        one.start()

    def signal(semaphore, dest):
        pl.semaphore_signal(semaphore, 1, device_id={"tm": dest}, device_id_type=MESH)

    barrier = pltpu.get_barrier_semaphore()
    signal(barrier, following)
    signal(barrier, preceding)

    def spread(level):
        step = 1 if level == 0 else 2 ** (level - 1)
        signal(ready.at[level], lax.rem(me + step, groups))
        signal(ready.at[level], lax.rem(me + groups - step, groups))

    def known(level):
        pl.semaphore_wait(ready.at[level], 2)

    def send(src, dst, dest, send_sem, recv_sem):
        return pltpu.make_async_remote_copy(
            src, dst, send_sem, recv_sem, device_id={"tm": dest}, device_id_type=MESH
        )

    def halo(s):
        return send(
            vbuf.at[s, pl.ds(blocks, 2)], vbuf.at[s, pl.ds(0, 2)], following, halo_send.at[s], halo_recv.at[s]
        )

    column, core = me // 2 % 4, me % 2
    plane = me // 8
    others = [
        lax.rem(plane + dz, 4) * 8 + lax.rem(column + dy, 4) * 2 + lax.rem(core + dc, 2)
        for dz, dy in FAR_FIRST for dc in (0, 1) if (dz, dy, dc) != (0, 0, 0)
    ]

    def split_taps():
        for jb in range(J // 8):
            t = [taps[pl.ds(jb * 64 + ((k // 8) * 256 + k % 8), 8, stride=8), :] for k in range(TAPS)]
            for i in range(half):
                half_taps[jb, i] = t[2 * i]
                half_taps[jb, half + i] = t[2 * i + 1]
                half_taps[jb, 2 * half + i] = t[2 * i] + t[2 * i + 1]

    def fir(first, count, s):
        pairs = count // 2
        base = first // 8

        @pl.loop(0, J // 8)
        def _(jb):
            def sample(g):
                return vbuf.at[s, base + (g + 16) // 8][pl.ds(jb * 64 + (g + 16) % 8, 8, stride=8), :]

            def run(h, x):
                total = h[0] * x[half - 1]
                for i in range(1, half):
                    total = total + h[i] * x[half - 1 - i]
                return total

            h = [half_taps[jb, i] for i in range(half)]
            x = [sample(2 * n) for n in range(1 - half, 0)]
            for n in range(1 - half, 0):
                xbuf[0, n + half] = x[n + half - 1]
            for n in range(pairs):
                x = (x + [sample(2 * n)])[-half:]
                xbuf[0, n + half] = x[-1]
                xbuf[1, n] = run(h, x)

            place = pl.ds(pl.multiple_of(s * J + jb * 8, 8), 8)
            h = [half_taps[jb, half + i] for i in range(half)]
            x = [sample(2 * n + 1) for n in range(-half, 0)]
            for n in range(1 - half, 0):
                xbuf[3, n + half] = x[n + half] + xbuf[0, n + half]
            before = run(h, x)
            for n in range(pairs):
                x = x[1:] + [sample(2 * n + 1)]
                xbuf[3, n + half] = x[-1] + xbuf[0, n + half]
                a, b = xbuf[1, n], run(h, x)
                ybuf[2 * n, place, :] = a + before
                xbuf[2, n] = a + b
                before = b

            h = [half_taps[jb, 2 * half + i] for i in range(half)]
            x = [xbuf[3, n + half] for n in range(1 - half, 0)]
            for n in range(pairs):
                x = (x + [xbuf[3, n + half]])[-half:]
                ybuf[2 * n + 1, place, :] = run(h, x) - xbuf[2, n]

    def first_stage(part):
        cosine, sine = twist[0], twist[1]
        for pair in range(4):
            f = part * 8 + pair * 2
            y = jnp.concatenate([ybuf[f], ybuf[f + 1]], axis=1)
            high, low = split(y)
            o = dot(outer[...], jnp.concatenate([high, low, high], axis=0))
            for h in range(2):
                re, im = o[:J, h * L:(h + 1) * L], o[J:, h * L:(h + 1) * L]
                z = jnp.concatenate([re * cosine + im * sine, im * cosine - re * sine], axis=1)
                place = pl.ds((pair * 2 + h) * J, J)
                zbuf[part, 0, place, :], zbuf[part, 1, place, :] = split(z)

    def second_stage(part):
        high, low = zbuf[part, 0], zbuf[part, 1]
        x = dot(high, inner[0]) + dot(low, inner[0]) + dot(high, inner[1])
        power = x[:, :L] * x[:, :L] + x[:, L:] * x[:, L:]
        for r in range(2):
            p = [power[(4 * r + f) * J:(4 * r + f + 1) * J] for f in range(4)]
            row = (p[0] + p[1]) + (p[2] + p[3])
            moments[0] += row
            moments[1] += (p[0] * p[0] + p[1] * p[1]) + (p[2] * p[2] + p[3] * p[3])
            held[part * 2 + r] = row

    def clean_lanes():
        block = lax.broadcasted_iota(jnp.int32, (groups, L), 0)
        lane = lax.broadcasted_iota(jnp.int32, (groups, L), 1)
        spread_out = jnp.where(lane // 4 == block, 1.0, 0.0)
        clean = jnp.broadcast_to(1.0 - flags[...].astype(F32), (8, groups))
        return dot(clean.astype(BF16), spread_out.astype(BF16))[0:1]

    def finish_rows(side, target):
        clean = moments[2, pl.ds(8, 1), :]
        scaled = []
        for a in range(4):
            row = held[side * 4 + a]
            part = jnp.sum(row, axis=0, keepdims=True) * clean
            total = jnp.sum(part, axis=1, keepdims=True)
            moments[2, pl.ds(0, 1), :] += part
            scaled.append(row * (clean * float(J * L)) * (1.0 / total))
        target[...] = owners_first(scaled).reshape(groups, 4, L)

    def send_wide(g):
        for dest in others:
            send(wide.at[g, dest], dyn.at[me, pl.ds(1 + 2 * g, 2)], dest, row_send, row_recv).start()

    def send_narrow():
        for dest in others:
            send(narrow.at[dest], dyn.at[me, 7], dest, row_send, row_recv).start()

    def spectra(parts, pending):
        first_stage(0)
        for action in pending:
            action()
        for part in range(1, parts):
            first_stage(part)
            second_stage(part - 1)
        second_stage(parts - 1)

    moments[...] = jnp.zeros_like(moments)

    loads[0].wait()
    split_taps()
    loads[1].wait()
    pl.semaphore_wait(barrier, 2)

    @pl.when(me < groups - 1)
    def _():
        halo(0).start()
        halo(1).start()

    spread(0)
    loads[2].wait()
    fir(16, 32, 0)
    known(0)
    spread(1)
    loads[3].wait()
    fir(16, 32, 1)
    known(1)
    spread(2)
    for piece in range(4, 10):
        loads[piece].wait()
    moments[2, pl.ds(8, 1), :] = clean_lanes()
    spectra(4, [])
    finish_rows(0, wide.at[0, :, 0])
    finish_rows(1, wide.at[0, :, 1])
    known(2)
    spread(3)
    fir(48, 32, 0)
    known(3)
    spread(4)
    fir(48, 32, 1)
    known(4)
    send_wide(0)
    spectra(4, [])
    finish_rows(0, wide.at[1, :, 0])
    finish_rows(1, wide.at[1, :, 1])
    send_wide(1)
    fir(80, 32, 0)
    fir(80, 32, 1)
    spectra(4, [])
    finish_rows(0, wide.at[2, :, 0])
    finish_rows(1, wide.at[2, :, 1])
    send_wide(2)
    fir(112, 16, 0)
    fir(112, 16, 1)
    spectra(2, [])
    finish_rows(0, narrow)
    send_narrow()

    for s in range(2):
        @pl.when(me > 0)
        def _():
            halo(s).wait_recv()

        @pl.when(me == 0)
        def _():
            vbuf[s, pl.ds(0, 2)] = jnp.zeros((2, 8 * J, L), F32)

        fir(0, 16, s)
    spectra(2, [])
    finish_rows(0, final.at[:, 0])

    local = jnp.sum(moments[2, pl.ds(0, 1), :], axis=1, keepdims=True)
    last = [moments[0], moments[1], jnp.broadcast_to(local, (J, L)), jnp.zeros((J, L), F32)]
    final[:, 1] = owners_first(last).reshape(groups, 4, L)
    for dest in others:
        send(final.at[dest], got.at[me], dest, fin_send, fin_recv).start()
    got[me] = final[me]
    for g in range(3):
        dyn[me, pl.ds(1 + 2 * g, 2)] = wide[g, me]
    dyn[me, 7] = narrow[me]

    everyone = pl.ds(0, groups - 1)
    send(final.at[everyone], got.at[everyone], following, fin_send, fin_recv).wait_recv()
    dyn[:, 0] = got[:, 0]
    sums = jnp.sum(got[:, 1], axis=0)
    first, second, group = sums[0:1], sums[1:2], sums[2:3]
    count = float(frames * groups)
    kurt[...] = (count + 1.0) / (count - 1.0) * (count * second / (first * first) - 1.0)
    lane = lax.broadcasted_iota(jnp.int32, (1, L), 1)
    mine = jnp.sum(jnp.where(lane == 4 * me, moments[2, pl.ds(8, 1), :], 0.0), axis=1, keepdims=True)
    spec[...] = float(J * L) * mine * first / group

    units = dyn.at[everyone, pl.ds(1, 7)]
    send(units, units, following, row_send, row_recv).wait()
    send(final.at[everyone], got.at[everyone], following, fin_send, fin_recv).wait_send()

    @pl.when(me < groups - 1)
    def _():
        halo(0).wait_send()
        halo(1).wait_send()


def body(groups, voltages, taps, flags):
    frames = voltages.shape[1]
    volt = voltages.reshape(2, frames // 8, 8, J, L).transpose(0, 1, 3, 2, 4).reshape(2, frames // 8, 8 * J, L)
    tap = taps.reshape(TAPS // 8, 8, J, L).transpose(0, 2, 1, 3).reshape(TAPS * J, L)
    outer, twist, inner = tables()
    vmem = pl.BlockSpec(memory_space=pltpu.VMEM)
    half = TAPS // 2
    operands = (volt, tap, flags.reshape(1, groups), jnp.asarray(outer), jnp.asarray(twist), jnp.asarray(inner))
    dyn, kurt, spec = pl.pallas_call(
        functools.partial(kernel, groups, frames),
        out_shape=(
            jax.ShapeDtypeStruct((groups, frames // 16, 4, L), F32),
            jax.ShapeDtypeStruct((1, L), F32),
            jax.ShapeDtypeStruct((1, L), F32),
        ),
        in_specs=[pl.BlockSpec(memory_space=pltpu.HBM)] * 6,
        out_specs=(vmem, vmem, vmem),
        scratch_shapes=[
            pltpu.VMEM((2, frames // 8 + 2, 8 * J, L), F32),
            pltpu.VMEM((TAPS * J, L), F32),
            pltpu.VMEM((1, groups), jnp.int32),
            pltpu.VMEM(outer.shape, BF16),
            pltpu.VMEM(twist.shape, F32),
            pltpu.VMEM(inner.shape, BF16),
            pltpu.VMEM((J // 8, 3 * half, 8, L), F32),
            pltpu.VMEM((4, CHUNK // 2 + half, 8, L), F32),
            pltpu.VMEM((CHUNK, 2 * J, L), F32),
            pltpu.VMEM((CHUNK // 8, 2, 8 * J, 2 * L), BF16),
            pltpu.VMEM((CHUNK // 4, J, L), F32),
            pltpu.VMEM((3, groups, 2, 4, L), F32),
            pltpu.VMEM((groups, 4, L), F32),
            pltpu.VMEM((groups, 2, 4, L), F32),
            pltpu.VMEM((3, J, L), F32),
            pltpu.VMEM((groups, 2, 4, L), F32),
            pltpu.SemaphoreType.DMA((10,)),
            pltpu.SemaphoreType.REGULAR((5,)),
            pltpu.SemaphoreType.DMA((2,)),
            pltpu.SemaphoreType.DMA((2,)),
        ] + [pltpu.SemaphoreType.DMA] * 4,
        compiler_params=pltpu.CompilerParams(
            collective_id=0, has_side_effects=True, vmem_limit_bytes=40 * 1024 * 1024
        ),
    )(*(pltpu.with_memory_space_constraint(x, pltpu.HBM) for x in operands))
    return dyn.reshape(groups * frames // 4, L), kurt.reshape(L), spec.reshape(L)


def solution(mesh):
    placed = (P(None, ("stream", "tm"), None), P(), P("stream"))
    return jax.shard_map(
        functools.partial(body, mesh.shape["tm"]),
        mesh=mesh,
        in_specs=placed,
        out_specs=(P("stream", "tm"), P(("stream", "tm")), P(("stream", "tm"))),
        check_vma=False,
    )
```

time: 30.6 us -> 33.4 us (1.092)
  Pallas kernels: 25.6 us -> 30.8 us
  local copies, waits for them, and re-layouts: 4.15 us -> 1.82 us
    pallas_call x1, Pallas kernels: 25.6 us -> 30.8 us  [body(): pl.pallas_call(functools.partial(kernel, groups, frames), out_shape=(jax....]
    unnamed x3, local copies, waits for them, and re-layouts: 4.15 us -> 1.82 us
where the time goes in v3:
time: 33.4 us; the launch traced here: 33.3 us
  Pallas kernels  30.8 us (92%)
  local copies, waits for them, and re-layouts  1.82 us (5%)
  between operations  0.64 us (2%)
    pallas_call x1, Pallas kernels, body(): pl.pallas_call(functools.partial(kernel, groups, frames), out_shape=(jax....  30.8 us
    unnamed x3, local copies, waits for them, and re-layouts  1.82 us

profile of v3, /device:TPU:1, one launch (start us, length us, event | category | flops | bytes accessed | tf_op | source)
XLA Modules:
  0.0 33.3 jit_solution(266298528765694581)
XLA Ops:
  0.6 30.8 %shard_map.85 = (f32[32,8,4,128]{3,2,1,0:T(4,128)S(1)}, f32[1,128]{1,0:T(1,128)S(1)}, f32[1,128]{1,0:T(1,128)S(1)}) custom-call(f32[2,16,256,128]{3,2,1,0:T(8,128)} %bitcast.17, f32[512,128]{1,0:T(8,128)} %bitcast.18, s32[1,32]{1,0:T(1,128)} %bitcast.19, bf16[64,192]{1,0:T(8,128)(2,1)} %constant.6.clone.outer_in, f32[2,32,128]{2,1,0:T(8,128)} %constant.7.clone.twist_in, ...), custom_call_target="tpu_custom_call" | custom-call | tf_op jit(solution)/shard_map/pallas_call | solution.py:355
  31.4 0.8 %copy.12 = f32[1024,128]{1,0:T(8,128)} copy(f32[1024,128]{1,0:T(8,128)S(1)} %bitcast.14) | data formatting | bytes 1048576
  32.2 0.5 %copy.13 = f32[128]{0:T(128)} copy(f32[128]{0:T(128)S(1)} %bitcast.16) | data formatting | bytes 1024
  32.7 0.5 %copy.14 = f32[128]{0:T(128)} copy(f32[128]{0:T(128)S(1)} %bitcast.15) | data formatting | bytes 1024

commit v4 on v3

--- a/solution.py
+++ b/solution.py
@@ -76,15 +76,15 @@
 def kernel(
     groups, frames,
     volt, taps_in, flags_in, outer_in, twist_in, inner_in,
-    dyn, kurt, spec,
-    vbuf, taps, flags, outer, twist, inner, half_taps, xbuf, ybuf, zbuf, held, wide, narrow, final, moments, got,
-    load_sem, ready, halo_send, halo_recv, row_send, row_recv, fin_send, fin_recv,
+    dyn, got, mine,
+    vbuf, taps, flags, outer, twist, inner, half_taps, xbuf, ybuf, zbuf, held, wide, narrow, final, moments,
+    load_sem, halo_send, halo_recv, row_send, row_recv, fin_send, fin_recv,
 ):
     me = lax.axis_index("tm")
     blocks = frames // 8
     half = TAPS // 2
     both = pl.ds(0, 2)
-    following, preceding = lax.rem(me + 1, groups), lax.rem(me + groups - 1, groups)
+    following = lax.rem(me + 1, groups)
 
     def load(piece, part, first, count):
         return pltpu.make_async_copy(
@@ -110,16 +110,8 @@
         pl.semaphore_signal(semaphore, 1, device_id={"tm": dest}, device_id_type=MESH)
 
     barrier = pltpu.get_barrier_semaphore()
-    signal(barrier, following)
-    signal(barrier, preceding)
-
-    def spread(level):
-        step = 1 if level == 0 else 2 ** (level - 1)
-        signal(ready.at[level], lax.rem(me + step, groups))
-        signal(ready.at[level], lax.rem(me + groups - step, groups))
-
-    def known(level):
-        pl.semaphore_wait(ready.at[level], 2)
+    for d in range(1, groups):
+        signal(barrier, lax.rem(me + d, groups))
 
     def send(src, dst, dest, send_sem, recv_sem):
         return pltpu.make_async_remote_copy(
@@ -146,55 +138,53 @@
                 half_taps[jb, half + i] = t[2 * i + 1]
                 half_taps[jb, 2 * half + i] = t[2 * i] + t[2 * i + 1]
 
-    def fir(first, count, s):
+    def fir(first, count, s, jb, slot):
         pairs = count // 2
-        base = first // 8
-
-        @pl.loop(0, J // 8)
-        def _(jb):
-            def sample(g):
-                return vbuf.at[s, base + (g + 16) // 8][pl.ds(jb * 64 + (g + 16) % 8, 8, stride=8), :]
-
-            def run(h, x):
-                total = h[0] * x[half - 1]
-                for i in range(1, half):
-                    total = total + h[i] * x[half - 1 - i]
-                return total
-
-            h = [half_taps[jb, i] for i in range(half)]
-            x = [sample(2 * n) for n in range(1 - half, 0)]
-            for n in range(1 - half, 0):
-                xbuf[0, n + half] = x[n + half - 1]
-            for n in range(pairs):
-                x = (x + [sample(2 * n)])[-half:]
-                xbuf[0, n + half] = x[-1]
-                xbuf[1, n] = run(h, x)
-
-            place = pl.ds(pl.multiple_of(s * J + jb * 8, 8), 8)
-            h = [half_taps[jb, half + i] for i in range(half)]
-            x = [sample(2 * n + 1) for n in range(-half, 0)]
-            for n in range(1 - half, 0):
-                xbuf[3, n + half] = x[n + half] + xbuf[0, n + half]
-            before = run(h, x)
-            for n in range(pairs):
-                x = x[1:] + [sample(2 * n + 1)]
-                xbuf[3, n + half] = x[-1] + xbuf[0, n + half]
-                a, b = xbuf[1, n], run(h, x)
-                ybuf[2 * n, place, :] = a + before
-                xbuf[2, n] = a + b
-                before = b
-
-            h = [half_taps[jb, 2 * half + i] for i in range(half)]
-            x = [xbuf[3, n + half] for n in range(1 - half, 0)]
-            for n in range(pairs):
-                x = (x + [xbuf[3, n + half]])[-half:]
-                ybuf[2 * n + 1, place, :] = run(h, x) - xbuf[2, n]
-
-    def first_stage(part):
+        keep = xbuf.at[jb % 2]
+
+        def sample(g):
+            return vbuf.at[s, (first + g + 16) // 8][pl.ds(jb * 64 + (g + 16) % 8, 8, stride=8), :]
+
+        def run(h, x):
+            total = h[0] * x[half - 1]
+            for i in range(1, half):
+                total = total + h[i] * x[half - 1 - i]
+            return total
+
+        h = [half_taps[jb, i] for i in range(half)]
+        x = [sample(2 * n) for n in range(1 - half, 0)]
+        for n in range(1 - half, 0):
+            keep[0, n + half] = x[n + half - 1]
+        for n in range(pairs):
+            x = (x + [sample(2 * n)])[-half:]
+            keep[0, n + half] = x[-1]
+            keep[1, n] = run(h, x)
+
+        place = pl.ds(s * J + jb * 8, 8)
+        h = [half_taps[jb, half + i] for i in range(half)]
+        x = [sample(2 * n + 1) for n in range(-half, 0)]
+        for n in range(1 - half, 0):
+            keep[3, n + half] = x[n + half] + keep[0, n + half]
+        before = run(h, x)
+        for n in range(pairs):
+            x = x[1:] + [sample(2 * n + 1)]
+            keep[3, n + half] = x[-1] + keep[0, n + half]
+            a, b = keep[1, n], run(h, x)
+            ybuf[slot, 2 * n, place, :] = a + before
+            keep[2, n] = a + b
+            before = b
+
+        h = [half_taps[jb, 2 * half + i] for i in range(half)]
+        x = [keep[3, n + half] for n in range(1 - half, 0)]
+        for n in range(pairs):
+            x = (x + [keep[3, n + half]])[-half:]
+            ybuf[slot, 2 * n + 1, place, :] = run(h, x) - keep[2, n]
+
+    def first_stage(part, slot):
         cosine, sine = twist[0], twist[1]
         for pair in range(4):
             f = part * 8 + pair * 2
-            y = jnp.concatenate([ybuf[f], ybuf[f + 1]], axis=1)
+            y = jnp.concatenate([ybuf[slot, f], ybuf[slot, f + 1]], axis=1)
             high, low = split(y)
             o = dot(outer[...], jnp.concatenate([high, low, high], axis=0))
             for h in range(2):
@@ -203,7 +193,7 @@
                 place = pl.ds((pair * 2 + h) * J, J)
                 zbuf[part, 0, place, :], zbuf[part, 1, place, :] = split(z)
 
-    def second_stage(part):
+    def second_stage(part, slot):
         high, low = zbuf[part, 0], zbuf[part, 1]
         x = dot(high, inner[0]) + dot(low, inner[0]) + dot(high, inner[1])
         power = x[:, :L] * x[:, :L] + x[:, L:] * x[:, L:]
@@ -212,7 +202,7 @@
             row = (p[0] + p[1]) + (p[2] + p[3])
             moments[0] += row
             moments[1] += (p[0] * p[0] + p[1] * p[1]) + (p[2] * p[2] + p[3] * p[3])
-            held[part * 2 + r] = row
+            held[slot, part * 2 + r] = row
 
     def clean_lanes():
         block = lax.broadcasted_iota(jnp.int32, (groups, L), 0)
@@ -221,11 +211,11 @@
         clean = jnp.broadcast_to(1.0 - flags[...].astype(F32), (8, groups))
         return dot(clean.astype(BF16), spread_out.astype(BF16))[0:1]
 
-    def finish_rows(side, target):
+    def finish_rows(slot, side, target):
         clean = moments[2, pl.ds(8, 1), :]
         scaled = []
         for a in range(4):
-            row = held[side * 4 + a]
+            row = held[slot, side * 4 + a]
             part = jnp.sum(row, axis=0, keepdims=True) * clean
             total = jnp.sum(part, axis=1, keepdims=True)
             moments[2, pl.ds(0, 1), :] += part
@@ -240,64 +230,61 @@
         for dest in others:
             send(narrow.at[dest], dyn.at[me, 7], dest, row_send, row_recv).start()
 
-    def spectra(parts, pending):
-        first_stage(0)
-        for action in pending:
+    pieces = [(s, jb) for s in range(2) for jb in range(J // 8)]
+
+    def stages(parts, slot):
+        order = [functools.partial(first_stage, 0, slot)]
+        for part in range(1, parts):
+            order.append(functools.partial(first_stage, part, slot))
+            order.append(functools.partial(second_stage, part - 1, slot))
+        return order + [functools.partial(second_stage, parts - 1, slot)]
+
+    def interleave(*lists):
+        keyed = [((n + 0.5) / len(one), k, action) for k, one in enumerate(lists) for n, action in enumerate(one)]
+        for _, _, action in sorted(keyed, key=lambda entry: entry[:2]):
             action()
-        for part in range(1, parts):
-            first_stage(part)
-            second_stage(part - 1)
-        second_stage(parts - 1)
+
+    def filters(first, count, slot):
+        return [functools.partial(fir, first, count, s, jb, slot) for s, jb in pieces]
 
     moments[...] = jnp.zeros_like(moments)
 
     loads[0].wait()
     split_taps()
+    loads[2].wait()
+    for action in filters(16, 32, 0)[:4]:
+        action()
+    loads[3].wait()
+    for action in filters(16, 32, 0)[4:]:
+        action()
     loads[1].wait()
-    pl.semaphore_wait(barrier, 2)
+    pl.semaphore_wait(barrier, groups - 1)
 
     @pl.when(me < groups - 1)
     def _():
         halo(0).start()
         halo(1).start()
 
-    spread(0)
-    loads[2].wait()
-    fir(16, 32, 0)
-    known(0)
-    spread(1)
-    loads[3].wait()
-    fir(16, 32, 1)
-    known(1)
-    spread(2)
     for piece in range(4, 10):
         loads[piece].wait()
     moments[2, pl.ds(8, 1), :] = clean_lanes()
-    spectra(4, [])
-    finish_rows(0, wide.at[0, :, 0])
-    finish_rows(1, wide.at[0, :, 1])
-    known(2)
-    spread(3)
-    fir(48, 32, 0)
-    known(3)
-    spread(4)
-    fir(48, 32, 1)
-    known(4)
-    send_wide(0)
-    spectra(4, [])
-    finish_rows(0, wide.at[1, :, 0])
-    finish_rows(1, wide.at[1, :, 1])
-    send_wide(1)
-    fir(80, 32, 0)
-    fir(80, 32, 1)
-    spectra(4, [])
-    finish_rows(0, wide.at[2, :, 0])
-    finish_rows(1, wide.at[2, :, 1])
-    send_wide(2)
-    fir(112, 16, 0)
-    fir(112, 16, 1)
-    spectra(2, [])
-    finish_rows(0, narrow)
+
+    def finish(g, side):
+        return functools.partial(finish_rows, g % 2, side, wide.at[g, :, side])
+
+    interleave(filters(48, 32, 1), stages(4, 0))
+    interleave(
+        filters(80, 32, 0),
+        stages(4, 1),
+        [finish(0, 0), finish(0, 1), functools.partial(send_wide, 0)],
+    )
+    interleave(
+        filters(112, 16, 1),
+        stages(4, 0),
+        [finish(1, 0), finish(1, 1), functools.partial(send_wide, 1)],
+    )
+    interleave(stages(2, 1), [finish(2, 0), finish(2, 1), functools.partial(send_wide, 2)])
+    finish_rows(1, 0, narrow)
     send_narrow()
 
     for s in range(2):
@@ -309,9 +296,10 @@
         def _():
             vbuf[s, pl.ds(0, 2)] = jnp.zeros((2, 8 * J, L), F32)
 
-        fir(0, 16, s)
-    spectra(2, [])
-    finish_rows(0, final.at[:, 0])
+        for action in filters(0, 16, 0)[4 * s:4 * s + 4]:
+            action()
+    interleave(stages(2, 0))
+    finish_rows(0, 0, final.at[:, 0])
 
     local = jnp.sum(moments[2, pl.ds(0, 1), :], axis=1, keepdims=True)
     last = [moments[0], moments[1], jnp.broadcast_to(local, (J, L)), jnp.zeros((J, L), F32)]
@@ -325,14 +313,9 @@
 
     everyone = pl.ds(0, groups - 1)
     send(final.at[everyone], got.at[everyone], following, fin_send, fin_recv).wait_recv()
-    dyn[:, 0] = got[:, 0]
-    sums = jnp.sum(got[:, 1], axis=0)
-    first, second, group = sums[0:1], sums[1:2], sums[2:3]
-    count = float(frames * groups)
-    kurt[...] = (count + 1.0) / (count - 1.0) * (count * second / (first * first) - 1.0)
     lane = lax.broadcasted_iota(jnp.int32, (1, L), 1)
-    mine = jnp.sum(jnp.where(lane == 4 * me, moments[2, pl.ds(8, 1), :], 0.0), axis=1, keepdims=True)
-    spec[...] = float(J * L) * mine * first / group
+    own = jnp.sum(jnp.where(lane == 4 * me, moments[2, pl.ds(8, 1), :], 0.0), axis=1, keepdims=True)
+    mine[...] = jnp.broadcast_to(own, (1, L))
 
     units = dyn.at[everyone, pl.ds(1, 7)]
     send(units, units, following, row_send, row_recv).wait()
@@ -342,6 +325,24 @@
     def _():
         halo(0).wait_send()
         halo(1).wait_send()
+
+
+def deliver(count, dyn, got, mine, rows, kurt, spec, kbuf, sbuf, sem):
+    later = pltpu.make_async_copy(dyn.at[:, pl.ds(1, 7)], rows.at[:, pl.ds(1, 7)], sem.at[0])
+    early = pltpu.make_async_copy(got.at[:, 0], rows.at[:, 0], sem.at[1])
+    later.start()
+    early.start()
+    sums = jnp.sum(got[:, 1], axis=0)
+    first, second, group = sums[0:1], sums[1:2], sums[2:3]
+    kbuf[...] = (count + 1.0) / (count - 1.0) * (count * second / (first * first) - 1.0)
+    sbuf[...] = float(J * L) * mine[...] * first / group
+    small = [pltpu.make_async_copy(kbuf, kurt, sem.at[2]), pltpu.make_async_copy(sbuf, spec, sem.at[3])]
+    for one in small:
+        one.start()
+    for one in small:
+        one.wait()
+    later.wait()
+    early.wait()
 
 
 def body(groups, voltages, taps, flags):
@@ -352,11 +353,11 @@
     vmem = pl.BlockSpec(memory_space=pltpu.VMEM)
     half = TAPS // 2
     operands = (volt, tap, flags.reshape(1, groups), jnp.asarray(outer), jnp.asarray(twist), jnp.asarray(inner))
-    dyn, kurt, spec = pl.pallas_call(
+    received = pl.pallas_call(
         functools.partial(kernel, groups, frames),
         out_shape=(
             jax.ShapeDtypeStruct((groups, frames // 16, 4, L), F32),
-            jax.ShapeDtypeStruct((1, L), F32),
+            jax.ShapeDtypeStruct((groups, 2, 4, L), F32),
             jax.ShapeDtypeStruct((1, L), F32),
         ),
         in_specs=[pl.BlockSpec(memory_space=pltpu.HBM)] * 6,
@@ -369,17 +370,15 @@
             pltpu.VMEM(twist.shape, F32),
             pltpu.VMEM(inner.shape, BF16),
             pltpu.VMEM((J // 8, 3 * half, 8, L), F32),
-            pltpu.VMEM((4, CHUNK // 2 + half, 8, L), F32),
-            pltpu.VMEM((CHUNK, 2 * J, L), F32),
+            pltpu.VMEM((2, 4, CHUNK // 2 + half, 8, L), F32),
+            pltpu.VMEM((2, CHUNK, 2 * J, L), F32),
             pltpu.VMEM((CHUNK // 8, 2, 8 * J, 2 * L), BF16),
-            pltpu.VMEM((CHUNK // 4, J, L), F32),
+            pltpu.VMEM((2, CHUNK // 4, J, L), F32),
             pltpu.VMEM((3, groups, 2, 4, L), F32),
             pltpu.VMEM((groups, 4, L), F32),
             pltpu.VMEM((groups, 2, 4, L), F32),
             pltpu.VMEM((3, J, L), F32),
-            pltpu.VMEM((groups, 2, 4, L), F32),
             pltpu.SemaphoreType.DMA((10,)),
-            pltpu.SemaphoreType.REGULAR((5,)),
             pltpu.SemaphoreType.DMA((2,)),
             pltpu.SemaphoreType.DMA((2,)),
         ] + [pltpu.SemaphoreType.DMA] * 4,
@@ -387,6 +386,19 @@
             collective_id=0, has_side_effects=True, vmem_limit_bytes=40 * 1024 * 1024
         ),
     )(*(pltpu.with_memory_space_constraint(x, pltpu.HBM) for x in operands))
+    hbm = pl.BlockSpec(memory_space=pltpu.HBM)
+    dyn, kurt, spec = pl.pallas_call(
+        functools.partial(deliver, float(frames * groups)),
+        out_shape=(
+            jax.ShapeDtypeStruct((groups, frames // 16, 4, L), F32),
+            jax.ShapeDtypeStruct((1, L), F32),
+            jax.ShapeDtypeStruct((1, L), F32),
+        ),
+        in_specs=[vmem] * 3,
+        out_specs=(hbm, hbm, hbm),
+        scratch_shapes=[pltpu.VMEM((1, L), F32), pltpu.VMEM((1, L), F32), pltpu.SemaphoreType.DMA((4,))],
+        compiler_params=pltpu.CompilerParams(vmem_limit_bytes=4 * 1024 * 1024),
+    )(*received)
     return dyn.reshape(groups * frames // 4, L), kurt.reshape(L), spec.reshape(L)
 
 

time: 33.4 us -> 24.5 us (0.73)
  Pallas kernels: 30.8 us -> 23.8 us
  local copies, waits for them, and re-layouts: 1.82 us -> 0 us
    pallas_call x1, Pallas kernels: 30.8 us -> 23 us  [body(): pl.pallas_call(functools.partial(kernel, groups, frames), out_shape=(jax....]
    unnamed x3 -> x0, local copies, waits for them, and re-layouts: 1.82 us -> none
    pallas_call x0 -> x1, Pallas kernels: none -> 0.82 us  [body(): pl.pallas_call(functools.partial(deliver, float(frames * groups)), out_sh...]
where the time goes in v4:
time: 24.5 us; the launch traced here: 24.4 us
  Pallas kernels  23.8 us (97%)
  between operations  0.64 us (3%)
    pallas_call x1, Pallas kernels, body(): pl.pallas_call(functools.partial(kernel, groups, frames), out_shape=(jax....  23 us
    pallas_call x1, Pallas kernels, body(): pl.pallas_call(functools.partial(deliver, float(frames * groups)), out_sh...  0.82 us

profile of v4, /device:TPU:1, one launch (start us, length us, event | category | flops | bytes accessed | tf_op | source)
XLA Modules:
  0.0 24.4 jit_solution(10816937166886468712)
XLA Ops:
  0.6 23.0 %shard_map.85 = (f32[32,8,4,128]{3,2,1,0:T(4,128)S(1)}, f32[32,2,4,128]{3,2,1,0:T(4,128)S(1)}, f32[1,128]{1,0:T(1,128)S(1)}) custom-call(f32[2,16,256,128]{3,2,1,0:T(8,128)} %bitcast.14, f32[512,128]{1,0:T(8,128)} %bitcast.15, s32[1,32]{1,0:T(1,128)} %bitcast.16, bf16[64,192]{1,0:T(8,128)(2,1)} %constant.6.clone.outer_in, ...), custom_call_target="tpu_custom_call" | custom-call | tf_op jit(solution)/shard_map/pallas_call | solution.py:356
  23.6 0.8 %shard_map.86 = (f32[32,8,4,128]{3,2,1,0:T(4,128)}, f32[1,128]{1,0:T(1,128)}, f32[1,128]{1,0:T(1,128)}) custom-call(f32[32,8,4,128]{3,2,1,0:T(4,128)S(1)} %get-tuple-element.9.dyn, f32[32,2,4,128]{3,2,1,0:T(4,128)S(1)} %get-tuple-element.10.got, f32[1,128]{1,0:T(1,128)S(1)} %get-tuple-element.11.mine), custom_call_target="tpu_custom_call" | custom-call | tf_op jit(solution)/shard_map/pallas_call | solution.py:390

commit v5 on v4

--- a/solution.py
+++ b/solution.py
@@ -78,7 +78,7 @@
     volt, taps_in, flags_in, outer_in, twist_in, inner_in,
     dyn, got, mine,
     vbuf, taps, flags, outer, twist, inner, half_taps, xbuf, ybuf, zbuf, held, wide, narrow, final, moments,
-    load_sem, halo_send, halo_recv, row_send, row_recv, fin_send, fin_recv,
+    load_sem, ready, halo_send, halo_recv, row_send, row_recv, fin_send, fin_recv,
 ):
     me = lax.axis_index("tm")
     blocks = frames // 8
@@ -110,8 +110,24 @@
         pl.semaphore_signal(semaphore, 1, device_id={"tm": dest}, device_id_type=MESH)
 
     barrier = pltpu.get_barrier_semaphore()
-    for d in range(1, groups):
-        signal(barrier, lax.rem(me + d, groups))
+    column, core, plane = me // 2 % 4, me % 2, me // 8
+    line = [plane * 8 + lax.rem(me + d, 8) for d in range(1, 8)]
+    across = [lax.rem(me + 8 * d, groups) for d in range(1, 4)]
+    for dest in line + across:
+        signal(barrier, dest)
+    ends = (lax.rem(me, 8) == 7, lax.rem(me, 8) == 0)
+
+    @pl.when(ends[0])
+    def _():
+        signal(barrier, following)
+
+    @pl.when(ends[1])
+    def _():
+        signal(barrier, lax.rem(me + groups - 1, groups))
+
+    def near_entered():
+        place = lax.rem(me, 8)
+        pl.semaphore_wait(barrier, 10 + lax.div(place, 7) + lax.div(7 - place, 7))
 
     def send(src, dst, dest, send_sem, recv_sem):
         return pltpu.make_async_remote_copy(
@@ -123,8 +139,6 @@
             vbuf.at[s, pl.ds(blocks, 2)], vbuf.at[s, pl.ds(0, 2)], following, halo_send.at[s], halo_recv.at[s]
         )
 
-    column, core = me // 2 % 4, me % 2
-    plane = me // 8
     others = [
         lax.rem(plane + dz, 4) * 8 + lax.rem(column + dy, 4) * 2 + lax.rem(core + dc, 2)
         for dz, dy in FAR_FIRST for dc in (0, 1) if (dz, dy, dc) != (0, 0, 0)
@@ -222,13 +236,20 @@
             scaled.append(row * (clean * float(J * L)) * (1.0 / total))
         target[...] = owners_first(scaled).reshape(groups, 4, L)
 
+    def in_turn(one, count):
+        def some(dests):
+            for dest in dests:
+                one(dest).start()
+
+        return [functools.partial(some, others[n::count]) for n in range(count)]
+
     def send_wide(g):
-        for dest in others:
-            send(wide.at[g, dest], dyn.at[me, pl.ds(1 + 2 * g, 2)], dest, row_send, row_recv).start()
-
-    def send_narrow():
-        for dest in others:
-            send(narrow.at[dest], dyn.at[me, 7], dest, row_send, row_recv).start()
+        return in_turn(
+            lambda dest: send(wide.at[g, dest], dyn.at[me, pl.ds(1 + 2 * g, 2)], dest, row_send, row_recv), 8
+        )
+
+    def send_narrow(count):
+        return in_turn(lambda dest: send(narrow.at[dest], dyn.at[me, 7], dest, row_send, row_recv), count)
 
     pieces = [(s, jb) for s in range(2) for jb in range(J // 8)]
 
@@ -251,20 +272,22 @@
 
     loads[0].wait()
     split_taps()
+    loads[1].wait()
+    near_entered()
+
+    @pl.when(me < groups - 1)
+    def _():
+        halo(0).start()
+        halo(1).start()
+
+    for dest in across:
+        signal(ready, dest)
     loads[2].wait()
     for action in filters(16, 32, 0)[:4]:
         action()
     loads[3].wait()
     for action in filters(16, 32, 0)[4:]:
         action()
-    loads[1].wait()
-    pl.semaphore_wait(barrier, groups - 1)
-
-    @pl.when(me < groups - 1)
-    def _():
-        halo(0).start()
-        halo(1).start()
-
     for piece in range(4, 10):
         loads[piece].wait()
     moments[2, pl.ds(8, 1), :] = clean_lanes()
@@ -272,20 +295,17 @@
     def finish(g, side):
         return functools.partial(finish_rows, g % 2, side, wide.at[g, :, side])
 
-    interleave(filters(48, 32, 1), stages(4, 0))
-    interleave(
-        filters(80, 32, 0),
-        stages(4, 1),
-        [finish(0, 0), finish(0, 1), functools.partial(send_wide, 0)],
-    )
-    interleave(
-        filters(112, 16, 1),
-        stages(4, 0),
-        [finish(1, 0), finish(1, 1), functools.partial(send_wide, 1)],
-    )
-    interleave(stages(2, 1), [finish(2, 0), finish(2, 1), functools.partial(send_wide, 2)])
-    finish_rows(1, 0, narrow)
-    send_narrow()
+    interleave(stages(4, 0))
+    interleave(filters(48, 32, 1))
+    pl.semaphore_wait(ready, 3)
+    interleave(stages(4, 1), [finish(0, 0), finish(0, 1)])
+    interleave(filters(80, 32, 0), send_wide(0))
+    interleave(stages(4, 0), [finish(1, 0), finish(1, 1)])
+    interleave(filters(112, 16, 1), send_wide(1))
+    interleave(stages(2, 1), [finish(2, 0), finish(2, 1)])
+    interleave(send_wide(2), [functools.partial(finish_rows, 1, 0, narrow)])
+    for action in send_narrow(1):
+        action()
 
     for s in range(2):
         @pl.when(me > 0)
@@ -379,6 +399,7 @@
             pltpu.VMEM((groups, 2, 4, L), F32),
             pltpu.VMEM((3, J, L), F32),
             pltpu.SemaphoreType.DMA((10,)),
+            pltpu.SemaphoreType.REGULAR,
             pltpu.SemaphoreType.DMA((2,)),
             pltpu.SemaphoreType.DMA((2,)),
         ] + [pltpu.SemaphoreType.DMA] * 4,

time: 24.5 us -> 23.4 us (0.955)
  Pallas kernels: 23.8 us -> 22.7 us
    pallas_call x1, Pallas kernels: 23 us -> 21.9 us  [body(): pl.pallas_call(functools.partial(kernel, groups, frames), out_shape=(jax....]
where the time goes in v5:
time: 23.4 us; the launch traced here: 23.3 us
  Pallas kernels  22.7 us (97%)
  between operations  0.64 us (3%)
    pallas_call x1, Pallas kernels, body(): pl.pallas_call(functools.partial(kernel, groups, frames), out_shape=(jax....  21.9 us
    pallas_call x1, Pallas kernels, body(): pl.pallas_call(functools.partial(deliver, float(frames * groups)), out_sh...  0.82 us

profile of v5, /device:TPU:1, one launch (start us, length us, event | category | flops | bytes accessed | tf_op | source)
XLA Modules:
  0.0 23.3 jit_solution(15961079019938737618)
XLA Ops:
  0.6 21.9 %shard_map.85 = (f32[32,8,4,128]{3,2,1,0:T(4,128)S(1)}, f32[32,2,4,128]{3,2,1,0:T(4,128)S(1)}, f32[1,128]{1,0:T(1,128)S(1)}) custom-call(f32[2,16,256,128]{3,2,1,0:T(8,128)} %bitcast.14, f32[512,128]{1,0:T(8,128)} %bitcast.15, s32[1,32]{1,0:T(1,128)} %bitcast.16, bf16[64,192]{1,0:T(8,128)(2,1)} %constant.6.clone.outer_in, ...), custom_call_target="tpu_custom_call" | custom-call | tf_op jit(solution)/shard_map/pallas_call | solution.py:376
  22.5 0.8 %shard_map.86 = (f32[32,8,4,128]{3,2,1,0:T(4,128)}, f32[1,128]{1,0:T(1,128)}, f32[1,128]{1,0:T(1,128)}) custom-call(f32[32,8,4,128]{3,2,1,0:T(4,128)S(1)} %get-tuple-element.9.dyn, f32[32,2,4,128]{3,2,1,0:T(4,128)S(1)} %get-tuple-element.10.got, f32[1,128]{1,0:T(1,128)S(1)} %get-tuple-element.11.mine), custom_call_target="tpu_custom_call" | custom-call | tf_op jit(solution)/shard_map/pallas_call | solution.py:411

commit v6 on v5

--- a/solution.py
+++ b/solution.py
@@ -69,20 +69,23 @@
     return rows
 
 
-def owners_first(rows):
-    return jnp.concatenate(exchange(rows), axis=0).T
+def owners_first(rows, scale=None):
+    rows = exchange(rows)
+    if scale is not None:
+        rows = [row * scale for row in rows]
+    return jnp.concatenate(rows, axis=0).T
 
 
 def kernel(
     groups, frames,
     volt, taps_in, flags_in, outer_in, twist_in, inner_in,
     dyn, got, mine,
-    vbuf, taps, flags, outer, twist, inner, half_taps, xbuf, ybuf, zbuf, held, wide, narrow, final, moments,
+    vbuf, taps, flags, outer, twist, inner, tap_sums, xbuf, ybuf, zbuf, held, wide, late, final, moments,
     load_sem, ready, halo_send, halo_recv, row_send, row_recv, fin_send, fin_recv,
 ):
     me = lax.axis_index("tm")
     blocks = frames // 8
-    half = TAPS // 2
+    quarter = TAPS // 4
     both = pl.ds(0, 2)
     following = lax.rem(me + 1, groups)
 
@@ -147,52 +150,79 @@
     def split_taps():
         for jb in range(J // 8):
             t = [taps[pl.ds(jb * 64 + ((k // 8) * 256 + k % 8), 8, stride=8), :] for k in range(TAPS)]
-            for i in range(half):
-                half_taps[jb, i] = t[2 * i]
-                half_taps[jb, half + i] = t[2 * i + 1]
-                half_taps[jb, 2 * half + i] = t[2 * i] + t[2 * i + 1]
+            for i in range(quarter):
+                a, b, c, d = t[4 * i:4 * i + 4]
+                for place, h in enumerate((a, c, a + c, b, d, b + d, a + b, c + d, (a + b) + (c + d))):
+                    tap_sums[jb, place, i] = h
 
     def fir(first, count, s, jb, slot):
-        pairs = count // 2
+        groups_of_four = count // 4
         keep = xbuf.at[jb % 2]
 
         def sample(g):
             return vbuf.at[s, (first + g + 16) // 8][pl.ds(jb * 64 + (g + 16) % 8, 8, stride=8), :]
 
         def run(h, x):
-            total = h[0] * x[half - 1]
-            for i in range(1, half):
-                total = total + h[i] * x[half - 1 - i]
+            total = h[0] * x[quarter - 1]
+            for i in range(1, quarter):
+                total = total + h[i] * x[quarter - 1 - i]
             return total
 
-        h = [half_taps[jb, i] for i in range(half)]
-        x = [sample(2 * n) for n in range(1 - half, 0)]
-        for n in range(1 - half, 0):
-            keep[0, n + half] = x[n + half - 1]
-        for n in range(pairs):
-            x = (x + [sample(2 * n)])[-half:]
-            keep[0, n + half] = x[-1]
-            keep[1, n] = run(h, x)
+        def nested(level, even, odd, give):
+            h = [[tap_sums[jb, 3 * level + k, i] for i in range(quarter)] for k in range(3)]
+            x = [even(n) for n in range(1 - quarter, 0)]
+            y = [odd(n) for n in range(-quarter, 0)]
+            z = [a + b for a, b in zip(x, y[1:])]
+            before = run(h[1], y)
+            for n in range(groups_of_four):
+                x, y = x[1 - quarter:] + [even(n)], y[1:] + [odd(n)]
+                z = z[1 - quarter:] + [x[-1] + y[-1]]
+                a, b, ab = run(h[0], x), run(h[1], y), run(h[2], z)
+                give(n, a + before, ab - (a + b))
+                before = b
 
         place = pl.ds(s * J + jb * 8, 8)
-        h = [half_taps[jb, half + i] for i in range(half)]
-        x = [sample(2 * n + 1) for n in range(-half, 0)]
-        for n in range(1 - half, 0):
-            keep[3, n + half] = x[n + half] + keep[0, n + half]
-        before = run(h, x)
-        for n in range(pairs):
-            x = x[1:] + [sample(2 * n + 1)]
-            keep[3, n + half] = x[-1] + keep[0, n + half]
-            a, b = keep[1, n], run(h, x)
-            ybuf[slot, 2 * n, place, :] = a + before
-            keep[2, n] = a + b
-            before = b
-
-        h = [half_taps[jb, 2 * half + i] for i in range(half)]
-        x = [keep[3, n + half] for n in range(1 - half, 0)]
-        for n in range(pairs):
-            x = (x + [keep[3, n + half]])[-half:]
-            ybuf[slot, 2 * n + 1, place, :] = run(h, x) - keep[2, n]
+        def even_samples(n, h):
+            value = sample(4 * n + 2 * h)
+            keep[0, 2 * n + h + 2 * quarter] = value
+            return value
+
+        def odd_samples(n, h):
+            value = sample(4 * n + 2 * h + 1)
+            keep[1, 2 * n + h + 2 * quarter] = value + keep[0, 2 * n + h + 2 * quarter]
+            return value
+
+        def sums(n, h):
+            return keep[1, 2 * n + h + 2 * quarter]
+
+        def give_even(n, u, v):
+            keep[2, 2 * n], keep[2, 2 * n + 1] = u, v
+
+        carried = []
+
+        def give_odd(n, u, v):
+            a, b = keep[2, 2 * n], keep[2, 2 * n + 1]
+            ybuf[slot, 4 * n, place, :] = a + carried[-1]
+            ybuf[slot, 4 * n + 2, place, :] = b + u
+            keep[3, 2 * n], keep[3, 2 * n + 1] = a + u, b + v
+            carried.append(v)
+
+        def give_sum(n, u, v):
+            ybuf[slot, 4 * n + 1, place, :] = u - keep[3, 2 * n]
+            ybuf[slot, 4 * n + 3, place, :] = v - keep[3, 2 * n + 1]
+
+        def start():
+            total = None
+            for i in range(quarter):
+                for k in range(2):
+                    term = tap_sums[jb, 3 + k, i] * sample(-1 - 4 * i - 2 * k)
+                    total = term if total is None else total + term
+            carried.append(total)
+
+        start()
+        nested(0, lambda n: even_samples(n, 0), lambda n: even_samples(n, 1), give_even)
+        nested(1, lambda n: odd_samples(n, 0), lambda n: odd_samples(n, 1), give_odd)
+        nested(2, lambda n: sums(n, 0), lambda n: sums(n, 1), give_sum)
 
     def first_stage(part, slot):
         cosine, sine = twist[0], twist[1]
@@ -227,14 +257,17 @@
 
     def finish_rows(slot, side, target):
         clean = moments[2, pl.ds(8, 1), :]
-        scaled = []
+        lane = lax.broadcasted_iota(jnp.int32, (1, L), 1)
+        rows, inverse, summed = [], None, None
         for a in range(4):
             row = held[slot, side * 4 + a]
             part = jnp.sum(row, axis=0, keepdims=True) * clean
-            total = jnp.sum(part, axis=1, keepdims=True)
-            moments[2, pl.ds(0, 1), :] += part
-            scaled.append(row * (clean * float(J * L)) * (1.0 / total))
-        target[...] = owners_first(scaled).reshape(groups, 4, L)
+            one = jnp.broadcast_to(1.0 / jnp.sum(part, axis=1, keepdims=True), (1, L))
+            inverse = one if a == 0 else jnp.where(lane % 4 == a, one, inverse)
+            summed = part if a == 0 else summed + part
+            rows.append(row * float(J * L))
+        moments[2, pl.ds(0, 1), :] += summed
+        target[...] = owners_first(rows, clean * inverse).reshape(groups, 4, L)
 
     def in_turn(one, count):
         def some(dests):
@@ -248,8 +281,8 @@
             lambda dest: send(wide.at[g, dest], dyn.at[me, pl.ds(1 + 2 * g, 2)], dest, row_send, row_recv), 8
         )
 
-    def send_narrow(count):
-        return in_turn(lambda dest: send(narrow.at[dest], dyn.at[me, 7], dest, row_send, row_recv), count)
+    def send_late():
+        return in_turn(lambda dest: send(late.at[dest], dyn.at[me, pl.ds(5, 3)], dest, row_send, row_recv), 8)
 
     pieces = [(s, jb) for s in range(2) for jb in range(J // 8)]
 
@@ -292,20 +325,19 @@
         loads[piece].wait()
     moments[2, pl.ds(8, 1), :] = clean_lanes()
 
-    def finish(g, side):
-        return functools.partial(finish_rows, g % 2, side, wide.at[g, :, side])
-
+    def finish(slot, side, target):
+        return functools.partial(finish_rows, slot, side, target)
+
+    interleave(filters(48, 32, 1))
     interleave(stages(4, 0))
-    interleave(filters(48, 32, 1))
+    interleave(stages(4, 1), [finish(0, side, wide.at[0, :, side]) for side in range(2)])
+    interleave(filters(80, 32, 0)[:2])
     pl.semaphore_wait(ready, 3)
-    interleave(stages(4, 1), [finish(0, 0), finish(0, 1)])
-    interleave(filters(80, 32, 0), send_wide(0))
-    interleave(stages(4, 0), [finish(1, 0), finish(1, 1)])
+    interleave(filters(80, 32, 0)[2:], [finish(1, side, wide.at[1, :, side]) for side in range(2)], send_wide(0))
     interleave(filters(112, 16, 1), send_wide(1))
-    interleave(stages(2, 1), [finish(2, 0), finish(2, 1)])
-    interleave(send_wide(2), [functools.partial(finish_rows, 1, 0, narrow)])
-    for action in send_narrow(1):
-        action()
+    interleave(stages(4, 0))
+    interleave(stages(2, 1), [finish(0, side, late.at[:, side]) for side in range(2)])
+    finish_rows(1, 0, late.at[:, 2])
 
     for s in range(2):
         @pl.when(me > 0)
@@ -316,8 +348,7 @@
         def _():
             vbuf[s, pl.ds(0, 2)] = jnp.zeros((2, 8 * J, L), F32)
 
-        for action in filters(0, 16, 0)[4 * s:4 * s + 4]:
-            action()
+        interleave(filters(0, 16, 0)[4 * s:4 * s + 4], [] if s else send_late())
     interleave(stages(2, 0))
     finish_rows(0, 0, final.at[:, 0])
 
@@ -327,9 +358,9 @@
     for dest in others:
         send(final.at[dest], got.at[me], dest, fin_send, fin_recv).start()
     got[me] = final[me]
-    for g in range(3):
+    for g in range(2):
         dyn[me, pl.ds(1 + 2 * g, 2)] = wide[g, me]
-    dyn[me, 7] = narrow[me]
+    dyn[me, pl.ds(5, 3)] = late[me]
 
     everyone = pl.ds(0, groups - 1)
     send(final.at[everyone], got.at[everyone], following, fin_send, fin_recv).wait_recv()
@@ -371,7 +402,6 @@
     tap = taps.reshape(TAPS // 8, 8, J, L).transpose(0, 2, 1, 3).reshape(TAPS * J, L)
     outer, twist, inner = tables()
     vmem = pl.BlockSpec(memory_space=pltpu.VMEM)
-    half = TAPS // 2
     operands = (volt, tap, flags.reshape(1, groups), jnp.asarray(outer), jnp.asarray(twist), jnp.asarray(inner))
     received = pl.pallas_call(
         functools.partial(kernel, groups, frames),
@@ -389,13 +419,13 @@
             pltpu.VMEM(outer.shape, BF16),
             pltpu.VMEM(twist.shape, F32),
             pltpu.VMEM(inner.shape, BF16),
-            pltpu.VMEM((J // 8, 3 * half, 8, L), F32),
-            pltpu.VMEM((2, 4, CHUNK // 2 + half, 8, L), F32),
+            pltpu.VMEM((J // 8, 9, TAPS // 4, 8, L), F32),
+            pltpu.VMEM((2, 4, CHUNK // 2 + TAPS // 2, 8, L), F32),
             pltpu.VMEM((2, CHUNK, 2 * J, L), F32),
             pltpu.VMEM((CHUNK // 8, 2, 8 * J, 2 * L), BF16),
             pltpu.VMEM((2, CHUNK // 4, J, L), F32),
-            pltpu.VMEM((3, groups, 2, 4, L), F32),
-            pltpu.VMEM((groups, 4, L), F32),
+            pltpu.VMEM((2, groups, 2, 4, L), F32),
+            pltpu.VMEM((groups, 3, 4, L), F32),
             pltpu.VMEM((groups, 2, 4, L), F32),
             pltpu.VMEM((3, J, L), F32),
             pltpu.SemaphoreType.DMA((10,)),

time: 23.4 us -> 23.4 us (level)
  no operation moved by 1% of the time
where the time goes in v6:
time: 23.4 us; the launch traced here: 23.3 us
  Pallas kernels  22.7 us (97%)
  between operations  0.64 us (3%)
    pallas_call x1, Pallas kernels, body(): pl.pallas_call(functools.partial(kernel, groups, frames), out_shape=(jax....  21.9 us
    pallas_call x1, Pallas kernels, body(): pl.pallas_call(functools.partial(deliver, float(frames * groups)), out_sh...  0.82 us

profile of v6, /device:TPU:1, one launch (start us, length us, event | category | flops | bytes accessed | tf_op | source)
XLA Modules:
  0.0 23.3 jit_solution(11927839456725619416)
XLA Ops:
  0.6 21.9 %shard_map.85 = (f32[32,8,4,128]{3,2,1,0:T(4,128)S(1)}, f32[32,2,4,128]{3,2,1,0:T(4,128)S(1)}, f32[1,128]{1,0:T(1,128)S(1)}) custom-call(f32[2,16,256,128]{3,2,1,0:T(8,128)} %bitcast.14, f32[512,128]{1,0:T(8,128)} %bitcast.15, s32[1,32]{1,0:T(1,128)} %bitcast.16, bf16[64,192]{1,0:T(8,128)(2,1)} %constant.6.clone.outer_in, ...), custom_call_target="tpu_custom_call" | custom-call | tf_op jit(solution)/shard_map/pallas_call | solution.py:406
  22.5 0.8 %shard_map.86 = (f32[32,8,4,128]{3,2,1,0:T(4,128)}, f32[1,128]{1,0:T(1,128)}, f32[1,128]{1,0:T(1,128)}) custom-call(f32[32,8,4,128]{3,2,1,0:T(4,128)S(1)} %get-tuple-element.9.dyn, f32[32,2,4,128]{3,2,1,0:T(4,128)S(1)} %get-tuple-element.10.got, f32[1,128]{1,0:T(1,128)S(1)} %get-tuple-element.11.mine), custom_call_target="tpu_custom_call" | custom-call | tf_op jit(solution)/shard_map/pallas_call | solution.py:441

commit v7 on v6

--- a/solution.py
+++ b/solution.py
@@ -106,15 +106,12 @@
         load(8, both, 6, 4),
         load(9, both, 10, 4),
     ]
-    for one in loads:
-        one.start()
-
     def signal(semaphore, dest):
         pl.semaphore_signal(semaphore, 1, device_id={"tm": dest}, device_id_type=MESH)
 
     barrier = pltpu.get_barrier_semaphore()
     column, core, plane = me // 2 % 4, me % 2, me // 8
-    line = [plane * 8 + lax.rem(me + d, 8) for d in range(1, 8)]
+    line = [plane * 8 + lax.rem(me + d, 8) for d in (1, 7, 2, 6, 3, 5, 4)]
     across = [lax.rem(me + 8 * d, groups) for d in range(1, 4)]
     for dest in line + across:
         signal(barrier, dest)
@@ -128,6 +125,9 @@
     def _():
         signal(barrier, lax.rem(me + groups - 1, groups))
 
+    for one in loads:
+        one.start()
+
     def near_entered():
         place = lax.rem(me, 8)
         pl.semaphore_wait(barrier, 10 + lax.div(place, 7) + lax.div(7 - place, 7))
@@ -137,9 +137,11 @@
             src, dst, send_sem, recv_sem, device_id={"tm": dest}, device_id_type=MESH
         )
 
-    def halo(s):
+    def halo(part):
+        s, rows = part // 2, pl.ds(part % 2 * 4 * J, 4 * J)
         return send(
-            vbuf.at[s, pl.ds(blocks, 2)], vbuf.at[s, pl.ds(0, 2)], following, halo_send.at[s], halo_recv.at[s]
+            vbuf.at[s, pl.ds(blocks, 2), rows], vbuf.at[s, pl.ds(0, 2), rows],
+            following, halo_send.at[part], halo_recv.at[part],
         )
 
     others = [
@@ -310,8 +312,8 @@
 
     @pl.when(me < groups - 1)
     def _():
-        halo(0).start()
-        halo(1).start()
+        for part in range(4):
+            halo(part).start()
 
     for dest in across:
         signal(ready, dest)
@@ -339,16 +341,17 @@
     interleave(stages(2, 1), [finish(0, side, late.at[:, side]) for side in range(2)])
     finish_rows(1, 0, late.at[:, 2])
 
-    for s in range(2):
+    @pl.when(me == 0)
+    def _():
+        vbuf[:, pl.ds(0, 2)] = jnp.zeros((2, 2, 8 * J, L), F32)
+
+    for part in range(4):
         @pl.when(me > 0)
         def _():
-            halo(s).wait_recv()
-
-        @pl.when(me == 0)
-        def _():
-            vbuf[s, pl.ds(0, 2)] = jnp.zeros((2, 8 * J, L), F32)
-
-        interleave(filters(0, 16, 0)[4 * s:4 * s + 4], [] if s else send_late())
+            halo(part).wait_recv()
+
+        interleave(filters(0, 16, 0)[2 * part:2 * part + 2], send_late()[4 * part:4 * part + 4])
+
     interleave(stages(2, 0))
     finish_rows(0, 0, final.at[:, 0])
 
@@ -374,8 +377,8 @@
 
     @pl.when(me < groups - 1)
     def _():
-        halo(0).wait_send()
-        halo(1).wait_send()
+        for part in range(4):
+            halo(part).wait_send()
 
 
 def deliver(count, dyn, got, mine, rows, kurt, spec, kbuf, sbuf, sem):
@@ -430,8 +433,8 @@
             pltpu.VMEM((3, J, L), F32),
             pltpu.SemaphoreType.DMA((10,)),
             pltpu.SemaphoreType.REGULAR,
-            pltpu.SemaphoreType.DMA((2,)),
-            pltpu.SemaphoreType.DMA((2,)),
+            pltpu.SemaphoreType.DMA((4,)),
+            pltpu.SemaphoreType.DMA((4,)),
         ] + [pltpu.SemaphoreType.DMA] * 4,
         compiler_params=pltpu.CompilerParams(
             collective_id=0, has_side_effects=True, vmem_limit_bytes=40 * 1024 * 1024

time: 23.4 us -> 23.5 us (level)
  no operation moved by 1% of the time
where the time goes in v7:
time: 23.5 us; the launch traced here: 23.3 us
  Pallas kernels  22.7 us (97%)
  between operations  0.64 us (3%)
    pallas_call x1, Pallas kernels, body(): pl.pallas_call(functools.partial(kernel, groups, frames), out_shape=(jax....  21.9 us
    pallas_call x1, Pallas kernels, body(): pl.pallas_call(functools.partial(deliver, float(frames * groups)), out_sh...  0.82 us

profile of v7, /device:TPU:1, one launch (start us, length us, event | category | flops | bytes accessed | tf_op | source)
XLA Modules:
  0.0 23.3 jit_solution(16715527657625554220)
XLA Ops:
  0.6 21.9 %shard_map.85 = (f32[32,8,4,128]{3,2,1,0:T(4,128)S(1)}, f32[32,2,4,128]{3,2,1,0:T(4,128)S(1)}, f32[1,128]{1,0:T(1,128)S(1)}) custom-call(f32[2,16,256,128]{3,2,1,0:T(8,128)} %bitcast.14, f32[512,128]{1,0:T(8,128)} %bitcast.15, s32[1,32]{1,0:T(1,128)} %bitcast.16, bf16[64,192]{1,0:T(8,128)(2,1)} %constant.6.clone.outer_in, ...), custom_call_target="tpu_custom_call" | custom-call | tf_op jit(solution)/shard_map/pallas_call | solution.py:409
  22.5 0.8 %shard_map.86 = (f32[32,8,4,128]{3,2,1,0:T(4,128)}, f32[1,128]{1,0:T(1,128)}, f32[1,128]{1,0:T(1,128)}) custom-call(f32[32,8,4,128]{3,2,1,0:T(4,128)S(1)} %get-tuple-element.9.dyn, f32[32,2,4,128]{3,2,1,0:T(4,128)S(1)} %get-tuple-element.10.got, f32[1,128]{1,0:T(1,128)S(1)} %get-tuple-element.11.mine), custom_call_target="tpu_custom_call" | custom-call | tf_op jit(solution)/shard_map/pallas_call | solution.py:444

commit v8 on v7

--- a/solution.py
+++ b/solution.py
@@ -340,6 +340,7 @@
     interleave(stages(4, 0))
     interleave(stages(2, 1), [finish(0, side, late.at[:, side]) for side in range(2)])
     finish_rows(1, 0, late.at[:, 2])
+    interleave(send_late())
 
     @pl.when(me == 0)
     def _():
@@ -350,7 +351,7 @@
         def _():
             halo(part).wait_recv()
 
-        interleave(filters(0, 16, 0)[2 * part:2 * part + 2], send_late()[4 * part:4 * part + 4])
+        interleave(filters(0, 16, 0)[2 * part:2 * part + 2])
 
     interleave(stages(2, 0))
     finish_rows(0, 0, final.at[:, 0])

time: 23.5 us -> 23.5 us (level)
  no operation moved by 1% of the time
where the time goes in v8:
time: 23.5 us; the launch traced here: 23.3 us
  Pallas kernels  22.7 us (97%)
  between operations  0.64 us (3%)
    pallas_call x1, Pallas kernels, body(): pl.pallas_call(functools.partial(kernel, groups, frames), out_shape=(jax....  21.9 us
    pallas_call x1, Pallas kernels, body(): pl.pallas_call(functools.partial(deliver, float(frames * groups)), out_sh...  0.82 us

profile of v8, /device:TPU:1, one launch (start us, length us, event | category | flops | bytes accessed | tf_op | source)
XLA Modules:
  0.0 23.3 jit_solution(15078675807339252704)
XLA Ops:
  0.6 21.9 %shard_map.85 = (f32[32,8,4,128]{3,2,1,0:T(4,128)S(1)}, f32[32,2,4,128]{3,2,1,0:T(4,128)S(1)}, f32[1,128]{1,0:T(1,128)S(1)}) custom-call(f32[2,16,256,128]{3,2,1,0:T(8,128)} %bitcast.14, f32[512,128]{1,0:T(8,128)} %bitcast.15, s32[1,32]{1,0:T(1,128)} %bitcast.16, bf16[64,192]{1,0:T(8,128)(2,1)} %constant.6.clone.outer_in, ...), custom_call_target="tpu_custom_call" | custom-call | tf_op jit(solution)/shard_map/pallas_call | solution.py:410
  22.5 0.8 %shard_map.86 = (f32[32,8,4,128]{3,2,1,0:T(4,128)}, f32[1,128]{1,0:T(1,128)}, f32[1,128]{1,0:T(1,128)}) custom-call(f32[32,8,4,128]{3,2,1,0:T(4,128)S(1)} %get-tuple-element.9.dyn, f32[32,2,4,128]{3,2,1,0:T(4,128)S(1)} %get-tuple-element.10.got, f32[1,128]{1,0:T(1,128)S(1)} %get-tuple-element.11.mine), custom_call_target="tpu_custom_call" | custom-call | tf_op jit(solution)/shard_map/pallas_call | solution.py:445

commit v9 on v8

--- a/solution.py
+++ b/solution.py
@@ -357,8 +357,10 @@
     finish_rows(0, 0, final.at[:, 0])
 
     local = jnp.sum(moments[2, pl.ds(0, 1), :], axis=1, keepdims=True)
-    last = [moments[0], moments[1], jnp.broadcast_to(local, (J, L)), jnp.zeros((J, L), F32)]
-    final[:, 1] = owners_first(last).reshape(groups, 4, L)
+    nothing = jnp.zeros((J, L), F32)
+    last = owners_first([moments[0], moments[1], nothing, nothing])
+    place = lax.broadcasted_iota(jnp.int32, last.shape, 0)
+    final[:, 1] = jnp.where(place % 4 == 2, local, last).reshape(groups, 4, L)
     for dest in others:
         send(final.at[dest], got.at[me], dest, fin_send, fin_recv).start()
     got[me] = final[me]
@@ -383,21 +385,23 @@
 
 
 def deliver(count, dyn, got, mine, rows, kurt, spec, kbuf, sbuf, sem):
-    later = pltpu.make_async_copy(dyn.at[:, pl.ds(1, 7)], rows.at[:, pl.ds(1, 7)], sem.at[0])
-    early = pltpu.make_async_copy(got.at[:, 0], rows.at[:, 0], sem.at[1])
-    later.start()
-    early.start()
+    quarter = dyn.shape[0] // 4
+    parts = [pl.ds(n * quarter, quarter) for n in range(4)]
+    large = [
+        pltpu.make_async_copy(dyn.at[part, pl.ds(1, 7)], rows.at[part, pl.ds(1, 7)], sem.at[n])
+        for n, part in enumerate(parts)
+    ] + [pltpu.make_async_copy(got.at[:, 0], rows.at[:, 0], sem.at[4])]
+    for one in large:
+        one.start()
     sums = jnp.sum(got[:, 1], axis=0)
     first, second, group = sums[0:1], sums[1:2], sums[2:3]
     kbuf[...] = (count + 1.0) / (count - 1.0) * (count * second / (first * first) - 1.0)
     sbuf[...] = float(J * L) * mine[...] * first / group
-    small = [pltpu.make_async_copy(kbuf, kurt, sem.at[2]), pltpu.make_async_copy(sbuf, spec, sem.at[3])]
+    small = [pltpu.make_async_copy(kbuf, kurt, sem.at[5]), pltpu.make_async_copy(sbuf, spec, sem.at[6])]
     for one in small:
         one.start()
-    for one in small:
+    for one in small + large:
         one.wait()
-    later.wait()
-    early.wait()
 
 
 def body(groups, voltages, taps, flags):
@@ -451,7 +455,7 @@
         ),
         in_specs=[vmem] * 3,
         out_specs=(hbm, hbm, hbm),
-        scratch_shapes=[pltpu.VMEM((1, L), F32), pltpu.VMEM((1, L), F32), pltpu.SemaphoreType.DMA((4,))],
+        scratch_shapes=[pltpu.VMEM((1, L), F32), pltpu.VMEM((1, L), F32), pltpu.SemaphoreType.DMA((7,))],
         compiler_params=pltpu.CompilerParams(vmem_limit_bytes=4 * 1024 * 1024),
     )(*received)
     return dyn.reshape(groups * frames // 4, L), kurt.reshape(L), spec.reshape(L)

time: 23.5 us -> 23.5 us (level)
  no operation moved by 1% of the time
where the time goes in v9:
time: 23.5 us; the launch traced here: 23.4 us
  Pallas kernels  22.7 us (97%)
  between operations  0.64 us (3%)
    pallas_call x1, Pallas kernels, body(): pl.pallas_call(functools.partial(kernel, groups, frames), out_shape=(jax....  21.9 us
    pallas_call x1, Pallas kernels, body(): pl.pallas_call(functools.partial(deliver, float(frames * groups)), out_sh...  0.85 us

profile of v9, /device:TPU:1, one launch (start us, length us, event | category | flops | bytes accessed | tf_op | source)
XLA Modules:
  0.0 23.4 jit_solution(6237102906994151556)
XLA Ops:
  0.6 21.9 %shard_map.85 = (f32[32,8,4,128]{3,2,1,0:T(4,128)S(1)}, f32[32,2,4,128]{3,2,1,0:T(4,128)S(1)}, f32[1,128]{1,0:T(1,128)S(1)}) custom-call(f32[2,16,256,128]{3,2,1,0:T(8,128)} %bitcast.14, f32[512,128]{1,0:T(8,128)} %bitcast.15, s32[1,32]{1,0:T(1,128)} %bitcast.16, bf16[64,192]{1,0:T(8,128)(2,1)} %constant.6.clone.outer_in, ...), custom_call_target="tpu_custom_call" | custom-call | tf_op jit(solution)/shard_map/pallas_call | solution.py:414
  22.5 0.8 %shard_map.86 = (f32[32,8,4,128]{3,2,1,0:T(4,128)}, f32[1,128]{1,0:T(1,128)}, f32[1,128]{1,0:T(1,128)}) custom-call(f32[32,8,4,128]{3,2,1,0:T(4,128)S(1)} %get-tuple-element.9.dyn, f32[32,2,4,128]{3,2,1,0:T(4,128)S(1)} %get-tuple-element.10.got, f32[1,128]{1,0:T(1,128)S(1)} %get-tuple-element.11.mine), custom_call_target="tpu_custom_call" | custom-call | tf_op jit(solution)/shard_map/pallas_call | solution.py:449
